TPU v7x, 256 devices: a whole 4x4x8 slice. The times are simulated.
256 devices in a mesh: row: 8 (over y, x_lo), col: 16 (over z, core), layer: 2 (over x_hi).
Axes of the slice: x: 4 (x_hi: 2, x_lo: 2; x = x_hi * 2 + x_lo), y: 4, z: 8, core: 2. Of those that a mesh axis runs over, the one named last changes fastest.
Arguments:
- tokens: bfloat16 [10240, 8192], P('row', 'col'), may hold values from -6 to 6
- up_weight: bfloat16 [8192, 16384], P('row', 'col'), may hold values from -0.0625 to 0.0625
Outputs:
- up: bfloat16 [10240, 16384], P('row', ('col', 'layer'))
All inputs are finite; a program needn't handle non-finite values.
Results may differ from a plain program's by a relative error of at most 0.001.
Values may be sent and summed in bfloat16 or wider, within the bound.
No kernel may reach another device: no remote copies, remote signals or barrier semaphores. Data moves between devices by JAX's collectives and lax.ppermute only.
A program may use at most 128 MiB of HBM per device.

v0:
```python
import jax
import jax.numpy as jnp
from jax import lax
from jax.sharding import Mesh
from jax.sharding import PartitionSpec as P

ROW = ("row_0", "row_1")


def gather_axes(shard, axes, dim):
    result = shard
    for number in range(len(axes) - 1, -1, -1):
        result = lax.all_gather(result, axes[number], axis=dim, tiled=True)
    return result


def per_device(tokens, up_weight):
    layers = lax.axis_size("layer")
    own_layer = lax.axis_index("layer")
    weight_height, weight_width = up_weight.shape
    half_width = weight_width // layers
    weight_part = lax.dynamic_slice_in_dim(up_weight, own_layer * half_width, half_width, 1)
    token_whole = lax.all_gather(tokens, "col", axis=1, tiled=True)
    partial_sum = jnp.dot(
        token_whole, gather_axes(weight_part, ROW, 0), preferred_element_type=jnp.float32
    )
    return partial_sum.astype(jnp.bfloat16)


def solution(mesh):
    split = Mesh(
        mesh.devices.reshape(4, 2, mesh.shape["col"], mesh.shape["layer"]),
        ("row_0", "row_1", "col", "layer"),
    )
    in_specs = (P(ROW, "col"), P(ROW, "col"))
    out_specs = P(ROW, ("col", "layer"))
    return jax.shard_map(
        per_device, mesh=split, in_specs=in_specs, out_specs=out_specs, check_vma=False
    )
```

profile of v0, /device:TPU:1, one launch (start us, length us, event | category | flops | bytes accessed | tf_op | source)
XLA Modules:
  0.0 282.9 jit_solution(16967732615238352690)
XLA Ops:
  6.5 0.0 copy-start
  6.5 0.0 all-gather.4.cloned.1.call-start
  6.5 1.6 copy-done
  8.1 1.1 constant_dynamic-slice_fusion
  9.2 0.0 all-gather.4.cloned.1.call-update
  9.2 0.0 all-gather.6.cloned.1.call-start
  9.3 41.9 %all-gather.4.cloned.1.call-done = bf16[2048,512]{1,0:T(8,128)(2,1)} async-done(((bf16[1024,512]{1,0:T(8,128)(2,1)}), bf16[2048,512]{1,0:T(8,128)(2,1)}) %all-gather.4.cloned.1.call-update) | async-done | bytes 2097168 | tf_op jit(solution)/shard_map/all_gather | solution.py:13
  51.2 0.0 all-gather.6.cloned.1.call-update
  51.2 0.0 all-gather.8.cloned.1.call-start
  51.2 0.7 all-gather.8.cloned.1.call-update
  51.9 87.7 %all-gather.6.cloned.1.call-done = bf16[8192,512]{1,0:T(8,128)(2,1)} async-done(((bf16[2048,512]{1,0:T(8,128)(2,1)}), bf16[8192,512]{1,0:T(8,128)(2,1)}) %all-gather.6.cloned.1.call-update) | async-done | bytes 8388624 | tf_op jit(solution)/shard_map/all_gather | solution.py:13
  139.6 118.5 %all-gather.8.cloned.1.call-done = bf16[1280,8192]{1,0:T(8,128)(2,1)} async-done(((bf16[1280,512]{1,0:T(8,128)(2,1)}), bf16[1280,8192]{1,0:T(8,128)(2,1)}) %all-gather.8.cloned.1.call-update) | async-done | bytes 20971536 | tf_op jit(solution)/shard_map/all_gather | solution.py:23
  258.2 16.7 %fusion = bf16[1280,512]{0,1:T(8,128)(2,1)S(1)} fusion(bf16[8192,512]{1,0:T(8,128)(2,1)} %all-gather.6.cloned.1.call-done, bf16[1280,8192]{1,0:T(8,128)(2,1)} %all-gather.8.cloned.1.call-done), kind=kOutput, calls=%fused_computation.1 | convolution fusion | flops 10738073600 | bytes 30670848 | tf_op jit(solution)/shard_map/dot_general | solution.py:24
  274.9 1.5 copy.3
Async XLA Ops:
  6.5 1.6 copy-start
  6.5 44.6 %all-gather.4.cloned.1.call-start = ((), (), s32[]{:S(2)}) async-start(), calls=%async_computation | async-start | bytes 3145728 | tf_op jit(solution)/shard_map/all_gather | solution.py:13
  9.2 130.4 %all-gather.6.cloned.1.call-start = ((), (), s32[]{:S(2)}) async-start(), calls=%async_computation.1 | async-start | bytes 10485760 | tf_op jit(solution)/shard_map/all_gather | solution.py:13
  51.2 207.0 %all-gather.8.cloned.1.call-start = ((), (), s32[]{:S(2)}) async-start(), calls=%async_computation.2 | async-start | bytes 22282240 | tf_op jit(solution)/shard_map/all_gather | solution.py:23
Sparse Core Ops, SparseCore 0:
  9.3 41.7 all-gather.3
  53.0 86.6 all-gather.5
  141.5 116.6 all-gather.7
where the time goes:
time: 283 us
  waiting for transfers between devices  249 us (88%)
  matrix products  16.7 us (6%)
  between operations  13.1 us (5%)
  local copies, waits for them, and re-layouts  4.14 us (1%)
    all_gather x2, waiting for transfers between devices, gather_axes(): result = lax.all_gather(result, axes[number], axis=dim, tiled=True)  130 us
    all_gather x1, waiting for transfers between devices, per_device(): token_whole = lax.all_gather(tokens, 'col', axis=1, tiled=True)  119 us
    dot_general x1, matrix products, per_device(): jnp.dot(token_whole, gather_axes(weight_part, ROW, 0), preferred_element_...  16.7 us
  transfers between devices with their start and end apart: 3, of which 3 were waited for; matrix products, arithmetic and copies ran while one was open for 0% of the time, Pallas kernels for 0%

commit v1 on v0

v1 whole, which is shorter than its diff:
```python
import jax
import jax.numpy as jnp
from jax import lax
from jax.sharding import Mesh
from jax.sharding import PartitionSpec as P


AXES = ("y", "xl", "z", "core", "xh")


def ring(size, shift):
    return [(i, (i + shift) % size) for i in range(size)]


def per_device(tokens, up_weight):
    y, xl, z, core, xh = (lax.axis_index(name) for name in AXES)
    zn, yn = lax.axis_size("z"), lax.axis_size("y")
    rows, depth = tokens.shape
    half = rows // 2
    width = up_weight.shape[1] // 2

    def zup(a):
        return lax.ppermute(a, "z", ring(zn, 1))

    def zdown(a):
        return lax.ppermute(a, "z", ring(zn, -1))

    def yup(a):
        return lax.ppermute(a, "y", ring(yn, 1))

    def ydown(a):
        return lax.ppermute(a, "y", ring(yn, -1))

    def peer(a):
        return lax.ppermute(a, "xh", ring(2, 1))

    mine = lax.dynamic_slice_in_dim(up_weight, core * depth, depth, 0)
    given = lax.dynamic_slice_in_dim(up_weight, (1 - core) * depth, depth, 0)

    own, oth = {}, {}
    own[0] = lax.dynamic_slice_in_dim(tokens, xh * half, half, 0)
    oth[0] = lax.dynamic_slice_in_dim(tokens, (1 - xh) * half, half, 0)
    own[-1] = zup(own[0])
    own[1] = zdown(own[0])
    got = lax.ppermute(given, "core", ring(2, 1))

    def both(part, layer):
        return jnp.concatenate(
            [lax.dynamic_slice_in_dim(a, layer * width, width, 1) for a in part], 1
        )

    quarter = depth // 2
    wa, wb = {}, {}
    wa[0] = both((mine, got), xh)
    far = both((mine[quarter:], got[quarter:]), 1 - xh)
    near_got = lax.ppermute(wa[0][:quarter], "xl", ring(2, 1))
    far_got = lax.ppermute(far, ("xl", "xh"), [(2, 1), (1, 2), (3, 0), (0, 3)])
    wa[-1] = yup(wa[0])
    wa[1] = ydown(wa[0])
    wb[0] = jnp.concatenate([near_got, far_got], 0)
    wb[-1] = yup(wb[0])
    wb[1] = ydown(wb[0])
    wa[2] = yup(wa[-1])
    wb[2] = ydown(wb[1])

    own[-2] = zup(own[-1])
    own[2] = zdown(own[1])
    own[-3] = zup(own[-2])
    own[3] = zdown(own[2])
    own[-4] = zup(own[-3])
    oth[1] = peer(own[1])
    oth[-1] = peer(own[-1])
    oth[-3] = peer(own[-3])
    oth[-4] = peer(own[-4])
    oth[2] = zdown(oth[1])
    oth[3] = zdown(oth[2])
    oth[-2] = zup(oth[-1])

    def gathered(pieces, order):
        buffer = jnp.zeros((half, zn * depth), tokens.dtype)
        for d in order:
            buffer = lax.dynamic_update_slice(buffer, pieces[d], (0, (d % zn) * depth))
        return buffer

    t_own = gathered(own, (0, -1, 1, -2, 2, -3, 3, -4))
    t_oth = gathered(oth, (0, 1, -1, 2, -3, -2, 3, -4))
    weight = jnp.zeros((zn * depth, 2 * width), up_weight.dtype)
    for pieces, side in ((wa, xl), (wb, 1 - xl)):
        for dy in (0, -1, 1, 2):
            block = 2 * ((y + dy) % yn) + side
            at = ((block - z) % zn) * depth
            weight = lax.dynamic_update_slice(weight, pieces[dy], (at, 0))
    w_own, w_partner = weight[:, :width], weight[:, width:]

    def dot(a, b):
        return jnp.dot(a, b, preferred_element_type=jnp.float32)

    sent_own = lax.ppermute(dot(t_own, w_partner), "core", ring(2, 1))
    sent_oth = lax.ppermute(dot(t_oth, w_partner), "core", ring(2, 1))
    r_own = (dot(t_own, w_own) + sent_own).astype(jnp.bfloat16)
    r_oth = (dot(t_oth, w_own) + sent_oth).astype(jnp.bfloat16)
    first = jnp.where(xh == 0, r_own, r_oth)
    second = jnp.where(xh == 0, r_oth, r_own)
    return jnp.concatenate([first, second], 0)


def solution(mesh):
    split = Mesh(
        mesh.devices.reshape(4, 2, mesh.shape["col"] // 2, 2, mesh.shape["layer"]), AXES
    )
    spec = P(("y", "xl"), ("z", "core"))
    return jax.shard_map(
        per_device,
        mesh=split,
        in_specs=(spec, spec),
        out_specs=P(("y", "xl"), ("z", "core", "xh")),
        check_vma=False,
    )
```

time: 283 us -> 183 us (0.65)
  waiting for transfers between devices: 249 us -> 66 us
  local copies, waits for them, and re-layouts: 4.14 us -> 46.2 us
  starting transfers between devices: 0.08 us -> 38.4 us
  between operations: 13.1 us -> 0.25 us
  matrix products: 16.7 us -> 28.6 us
  other arithmetic: 0 us -> 2.86 us
    all_gather x3 -> x0, waiting for transfers between devices: 248 us -> none  [the longest x2 130 us: gather_axes(): result = lax.all_gather(result, axes[number], axis=dim, tiled=True)]
    ppermute x0 -> x25, waiting for transfers between devices: none -> 66 us  [the longest x3 25 us: yup(): return lax.ppermute(a, 'y', ring(yn, 1))]
    ppermute x0 -> x25, starting transfers between devices: none -> 38.4 us  [the longest x5 9.61 us: zdown(): return lax.ppermute(a, 'z', ring(zn, -1))]
    dynamic_update_slice x0 -> x23, local copies, waits for them, and re-layouts: none -> 32.4 us  [the longest x16 22.5 us: gathered(): buffer = lax.dynamic_update_slice(buffer, pieces[d], (0, d % zn * depth))]
    dot_general x1 -> x4, matrix products: 16.7 us -> 28.6 us  [dot(): return jnp.dot(a, b, preferred_element_type=jnp.float32)]
    dynamic_slice x1 -> x6, local copies, waits for them, and re-layouts: 1.07 us -> 6.13 us  [the longest x4 3.47 us: both(): lax.dynamic_slice_in_dim(a, layer * width, width, 1)]
    broadcast_in_dim x0 -> x1, local copies, waits for them, and re-layouts: none -> 4.35 us  [per_device(): weight = jnp.zeros((zn * depth, 2 * width), up_weight.dtype)]
    concatenate x0 -> x4, other arithmetic: none -> 2.85 us  [the longest x3 1.71 us: both(): jnp.concatenate([lax.dynamic_slice_in_dim(a, layer * width, width, 1) for...]
  transfers between devices with their start and end apart: 3 -> 25, of which waited for: 3 -> 10; matrix products, arithmetic and copies ran while one was open for 0% -> 33% of each run, Pallas kernels for 0% -> 0%
where the time goes in v1:
time: 183 us; the launch traced here: 182 us
  waiting for transfers between devices  66 us (36%)
  local copies, waits for them, and re-layouts  46.2 us (25%)
  starting transfers between devices  38.4 us (21%)
  matrix products  28.6 us (16%)
  other arithmetic  2.86 us (2%)
    dot_general x4, matrix products, dot(): return jnp.dot(a, b, preferred_element_type=jnp.float32)  28.6 us
    ppermute x3, waiting for transfers between devices, yup(): return lax.ppermute(a, 'y', ring(yn, 1))  25 us
    dynamic_update_slice x16, local copies, waits for them, and re-layouts, gathered(): buffer = lax.dynamic_update_slice(buffer, pieces[d], (0, d % zn * depth))  22.5 us
    ppermute x5, waiting for transfers between devices, zup(): return lax.ppermute(a, 'z', ring(zn, 1))  21.4 us
    ppermute x4, waiting for transfers between devices, peer(): return lax.ppermute(a, 'xh', ring(2, 1))  15.9 us
    dynamic_update_slice x7, local copies, waits for them, and re-layouts, per_device(): weight = lax.dynamic_update_slice(weight, pieces[dy], (at, 0))  9.96 us
    ppermute x5, starting transfers between devices, zdown(): return lax.ppermute(a, 'z', ring(zn, -1))  9.61 us
    ppermute x3, starting transfers between devices, ydown(): return lax.ppermute(a, 'y', ring(yn, -1))  8.1 us
  transfers between devices with their start and end apart: 25, of which 10 were waited for; matrix products, arithmetic and copies ran while one was open for 33% of the time, Pallas kernels for 0%

profile of v1, /device:TPU:1, one launch (start us, length us, event | category | flops | bytes accessed | tf_op | source)
XLA Modules:
  0.0 182.2 jit_solution(13587025175086195153)
XLA Ops:
  0.0 1.3 constant_dynamic-slice_fusion.3
  1.3 3.3 %collective-permute-start.7 = (bf16[512,1024]{1,0:T(8,128)(2,1)S(1)}, bf16[512,1024]{1,0:T(8,128)(2,1)}, u32[]{:S(2)}, u32[]{:S(2)}) collective-permute-start(bf16[512,1024]{1,0:T(8,128)(2,1)S(1)} %constant_dynamic-slice_fusion.3), channel_id=1, source_target_pairs={{0,2},{2,0},{1,3},{3,1},{4,6},{6,4},{5,7},{7,5},{8,10},{10,8},{9,1... | collective-permute-start | bytes 3145736 | tf_op jit(solution)/shard_map/ppermute | solution.py:45
  4.6 1.4 constant_dynamic-slice_fusion.4
  6.0 3.9 %collective-permute-start.1 = (bf16[640,512]{1,0:T(8,128)(2,1)S(1)}, bf16[640,512]{1,0:T(8,128)(2,1)}, u32[]{:S(2)}, u32[]{:S(2)}) collective-permute-start(bf16[640,512]{1,0:T(8,128)(2,1)S(1)} %get-tuple-element.7), channel_id=1, source_target_pairs={{0,28},{4,0},{8,4},{12,8},{16,12},{20,16},{24,20},{28,24},{1,29},{... | collective-permute-start | bytes 1966088 | tf_op jit(solution)/shard_map/ppermute | solution.py:26
  10.0 15.1 %collective-permute-done = bf16[640,512]{1,0:T(8,128)(2,1)} collective-permute-done((bf16[640,512]{1,0:T(8,128)(2,1)S(1)}, bf16[640,512]{1,0:T(8,128)(2,1)}, u32[]{:S(2)}, u32[]{:S(2)}) %collective-permute-start) | collective-permute-done | bytes 655392 | tf_op jit(solution)/shard_map/ppermute | solution.py:23
  25.1 2.7 %collective-permute-start.3 = (bf16[640,512]{1,0:T(8,128)(2,1)}, bf16[640,512]{1,0:T(8,128)(2,1)}, u32[]{:S(2)}, u32[]{:S(2)}) collective-permute-start(bf16[640,512]{1,0:T(8,128)(2,1)} %collective-permute-done.1), channel_id=1, source_target_pairs={{0,28},{4,0},{8,4},{12,8},{16,12},{20,16},{24,20},{28,24},{1,29},{... | collective-permute-start | bytes 1966088 | tf_op jit(solution)/shard_map/ppermute | solution.py:26
  27.8 1.4 dynamic_slice.25
  30.2 1.1 slice.22
  31.3 2.5 %collective-permute-start.12 = (bf16[256,1024]{1,0:T(8,128)(2,1)S(1)}, bf16[256,1024]{1,0:T(8,128)(2,1)}, u32[]{:S(2)}, u32[]{:S(2)}) collective-permute-start(bf16[256,1024]{1,0:T(8,128)(2,1)S(1)} %pad_maximum_fusion.2), channel_id=1, source_target_pairs={{32,1},{1,32},{33,0},{0,33},{34,3},{3,34},{35,2},{2,35},{36,5},{5,... | collective-permute-start | bytes 1572872 | tf_op jit(solution)/shard_map/ppermute | solution.py:57
  35.1 1.4 collective-permute-start.17
  36.5 5.8 %collective-permute-done.2 = bf16[640,512]{1,0:T(8,128)(2,1)} collective-permute-done((bf16[640,512]{1,0:T(8,128)(2,1)}, bf16[640,512]{1,0:T(8,128)(2,1)}, u32[]{:S(2)}, u32[]{:S(2)}) %collective-permute-start.2) | collective-permute-done | bytes 655392 | tf_op jit(solution)/shard_map/ppermute | solution.py:23
  42.3 2.7 %collective-permute-start.18 = (bf16[640,512]{1,0:T(8,128)(2,1)}, bf16[640,512]{1,0:T(8,128)(2,1)}, u32[]{:S(2)}, u32[]{:S(2)}) collective-permute-start(bf16[640,512]{1,0:T(8,128)(2,1)} %collective-permute-done), channel_id=1, source_target_pairs={{0,1},{1,0},{2,3},{3,2},{4,5},{5,4},{6,7},{7,6},{8,9},{9,8},{10,11... | collective-permute-start | bytes 1966088 | tf_op jit(solution)/shard_map/ppermute | solution.py:35
  45.1 2.7 %collective-permute-start.5 = (bf16[640,512]{1,0:T(8,128)(2,1)}, bf16[640,512]{1,0:T(8,128)(2,1)}, u32[]{:S(2)}, u32[]{:S(2)}) collective-permute-start(bf16[640,512]{1,0:T(8,128)(2,1)} %collective-permute-done.3), channel_id=1, source_target_pairs={{0,28},{4,0},{8,4},{12,8},{16,12},{20,16},{24,20},{28,24},{1,29},{... | collective-permute-start | bytes 1966088 | tf_op jit(solution)/shard_map/ppermute | solution.py:26
  47.7 4.4 %broadcast_in_dim.3 = bf16[4096,1024]{1,0:T(8,128)(2,1)} broadcast(bf16[]{:T(256)} %constant.111.clone.1), dimensions={} | broadcast | bytes 8388610 | tf_op jit(solution)/shard_map/broadcast_in_dim | solution.py:87
  52.1 1.6 pad_maximum_fusion.1
  53.7 1.3 collective-permute-start.8
  56.1 1.1 constant_dynamic-update-slice_fusion.22
  57.1 4.0 %collective-permute-done.17 = bf16[640,512]{1,0:T(8,128)(2,1)S(1)} collective-permute-done((bf16[640,512]{1,0:T(8,128)(2,1)}, bf16[640,512]{1,0:T(8,128)(2,1)S(1)}, u32[]{:S(2)}, u32[]{:S(2)}) %collective-permute-start.17) | collective-permute-done | bytes 655392 | tf_op jit(solution)/shard_map/ppermute | solution.py:35
  61.1 2.7 %collective-permute-start.9 = (bf16[512,1024]{1,0:T(8,128)(2,1)}, bf16[512,1024]{1,0:T(8,128)(2,1)}, u32[]{:S(2)}, u32[]{:S(2)}) collective-permute-start(bf16[512,1024]{1,0:T(8,128)(2,1)} %get-tuple-element.9), channel_id=1, source_target_pairs={{0,192},{64,0},{128,64},{192,128},{1,193},{65,1},{129,65},{193,129... | collective-permute-start | bytes 3145736 | tf_op jit(solution)/shard_map/ppermute | solution.py:32
  63.9 11.4 %collective-permute-done.18 = bf16[640,512]{1,0:T(8,128)(2,1)} collective-permute-done((bf16[640,512]{1,0:T(8,128)(2,1)}, bf16[640,512]{1,0:T(8,128)(2,1)}, u32[]{:S(2)}, u32[]{:S(2)}) %collective-permute-start.18) | collective-permute-done | bytes 655392 | tf_op jit(solution)/shard_map/ppermute | solution.py:35
  75.3 2.7 %collective-permute-start.14 = (bf16[512,1024]{1,0:T(8,128)(2,1)S(1)}, bf16[512,1024]{1,0:T(8,128)(2,1)S(1)}, u32[]{:S(2)}, u32[]{:S(2)}) collective-permute-start(bf16[512,1024]{1,0:T(8,128)(2,1)S(1)} %constant_dynamic-update-slice_fusion.22), channel_id=1, source_target_pairs={{0,192},{64,0},{128,64},{192,128},{1,193},{65,1},{129,65},{193,129... | collective-permute-start | bytes 3145736 | tf_op jit(solution)/shard_map/ppermute | solution.py:32
  78.0 2.9 %dynamic_update_slice.72 = bf16[640,4096]{1,0:T(8,128)(2,1)} pad(bf16[640,512]{1,0:T(8,128)(2,1)S(1)} %get-tuple-element.7, bf16[]{:T(256)} %constant.111.clone.1), padding=0_0x0_3584 | pad | bytes 5898242 | tf_op jit(solution)/shard_map/dynamic_update_slice | solution.py:82
  81.0 3.0 %dynamic_update_slice.88 = bf16[640,4096]{1,0:T(8,128)(2,1)} pad(bf16[640,512]{1,0:T(8,128)(2,1)S(1)} %get-tuple-element.8, bf16[]{:T(256)} %constant.111.clone.1), padding=0_0x0_3584 | pad | bytes 5898242 | tf_op jit(solution)/shard_map/dynamic_update_slice | solution.py:82
  84.0 2.0 %constant_dynamic-update-slice_fusion.21 = bf16[640,4096]{1,0:T(8,128)(2,1)} fusion(bf16[640,4096]{1,0:T(8,128)(2,1)} %dynamic_update_slice.72, bf16[640,512]{1,0:T(8,128)(2,1)} %collective-permute-done), kind=kLoop, calls=%fused_computation.45 | loop fusion | bytes 1310720 | tf_op jit(solution)/shard_map/dynamic_update_slice | solution.py:82
  86.0 1.5 collective-permute-start.21
  87.5 2.0 %constant_dynamic-update-slice_fusion.20 = bf16[640,4096]{1,0:T(8,128)(2,1)} fusion(bf16[640,4096]{1,0:T(8,128)(2,1)} %constant_dynamic-update-slice_fusion.21, bf16[640,512]{1,0:T(8,128)(2,1)} %collective-permute-done.1), kind=kLoop, calls=%fused_computation.44 | loop fusion | bytes 1310720 | tf_op jit(solution)/shard_map/dynamic_update_slice | solution.py:82
  89.5 2.0 %constant_dynamic-update-slice_fusion.19 = bf16[640,4096]{1,0:T(8,128)(2,1)} fusion(bf16[640,4096]{1,0:T(8,128)(2,1)} %constant_dynamic-update-slice_fusion.20, bf16[640,512]{1,0:T(8,128)(2,1)} %collective-permute-done.2), kind=kLoop, calls=%fused_computation.43 | loop fusion | bytes 1310720 | tf_op jit(solution)/shard_map/dynamic_update_slice | solution.py:82
  91.5 2.0 %constant_dynamic-update-slice_fusion.18 = bf16[640,4096]{1,0:T(8,128)(2,1)} fusion(bf16[640,4096]{1,0:T(8,128)(2,1)} %constant_dynamic-update-slice_fusion.19, bf16[640,512]{1,0:T(8,128)(2,1)} %collective-permute-done.3), kind=kLoop, calls=%fused_computation.42 | loop fusion | bytes 1310720 | tf_op jit(solution)/shard_map/dynamic_update_slice | solution.py:82
  94.5 2.0 %constant_dynamic-update-slice_fusion.4 = bf16[640,4096]{1,0:T(8,128)(2,1)} fusion(bf16[640,4096]{1,0:T(8,128)(2,1)} %constant_dynamic-update-slice_fusion.5, bf16[640,512]{1,0:T(8,128)(2,1)} %collective-permute-done.18), kind=kLoop, calls=%fused_computation.24 | loop fusion | bytes 1310720 | tf_op jit(solution)/shard_map/dynamic_update_slice | solution.py:82
  96.5 1.2 collective-permute-done.19
  97.7 1.7 collective-permute-start.20
  99.4 2.1 %constant_dynamic-update-slice_fusion.17 = bf16[640,4096]{1,0:T(8,128)(2,1)} fusion(bf16[640,4096]{1,0:T(8,128)(2,1)} %constant_dynamic-update-slice_fusion.18, bf16[640,512]{1,0:T(8,128)(2,1)} %collective-permute-done.4), kind=kLoop, calls=%fused_computation.41 | loop fusion | bytes 1310720 | tf_op jit(solution)/shard_map/dynamic_update_slice | solution.py:82
  102.4 2.4 %collective-permute-done.14 = bf16[512,1024]{1,0:T(8,128)(2,1)S(1)} collective-permute-done((bf16[512,1024]{1,0:T(8,128)(2,1)S(1)}, bf16[512,1024]{1,0:T(8,128)(2,1)S(1)}, u32[]{:S(2)}, u32[]{:S(2)}) %collective-permute-start.14) | collective-permute-done | bytes 1048608 | tf_op jit(solution)/shard_map/ppermute | solution.py:32
  105.2 2.1 %constant_dynamic-update-slice_fusion.16 = bf16[640,4096]{1,0:T(8,128)(2,1)} fusion(bf16[640,4096]{1,0:T(8,128)(2,1)} %constant_dynamic-update-slice_fusion.17, bf16[640,512]{1,0:T(8,128)(2,1)} %collective-permute-done.5), kind=kLoop, calls=%fused_computation.40 | loop fusion | bytes 1310720 | tf_op jit(solution)/shard_map/dynamic_update_slice | solution.py:82
  107.3 2.3 %constant_dynamic-update-slice_fusion.13 = bf16[4096,1024]{1,0:T(8,128)(2,1)} fusion(bf16[4096,1024]{1,0:T(8,128)(2,1)} %get-tuple-element.10, bf16[512,1024]{1,0:T(8,128)(2,1)} %collective-permute-done.8, s32[]{:T(128)S(6)} %select_n.131), kind=kLoop, calls=%fused_computation.35 | loop fusion | bytes 2097156 | tf_op jit(solution)/shard_map/dynamic_update_slice | solution.py:92
  109.5 2.3 %constant_dynamic-update-slice_fusion.12 = bf16[4096,1024]{1,0:T(8,128)(2,1)} fusion(bf16[4096,1024]{1,0:T(8,128)(2,1)} %constant_dynamic-update-slice_fusion.13, bf16[512,1024]{1,0:T(8,128)(2,1)} %collective-permute-done.9, s32[]{:T(128)S(6)} %select_n.134), kind=kLoop, calls=%fused_computation.34 | loop fusion | bytes 2097156 | tf_op jit(solution)/shard_map/dynamic_update_slice | solution.py:92
  112.3 2.6 %collective-permute-start.15 = (bf16[512,1024]{1,0:T(8,128)(2,1)S(1)}, bf16[512,1024]{1,0:T(8,128)(2,1)S(1)}, u32[]{:S(2)}, u32[]{:S(2)}) collective-permute-start(bf16[512,1024]{1,0:T(8,128)(2,1)S(1)} %collective-permute-done.14), channel_id=1, source_target_pairs={{0,192},{64,0},{128,64},{192,128},{1,193},{65,1},{129,65},{193,129... | collective-permute-start | bytes 3145736 | tf_op jit(solution)/shard_map/ppermute | solution.py:32
  115.6 1.5 collective-permute-start.23
  117.3 4.6 %collective-permute-done.10 = bf16[512,1024]{1,0:T(8,128)(2,1)S(1)} collective-permute-done((bf16[512,1024]{1,0:T(8,128)(2,1)}, bf16[512,1024]{1,0:T(8,128)(2,1)S(1)}, u32[]{:S(2)}, u32[]{:S(2)}) %collective-permute-start.10) | collective-permute-done | bytes 1048608 | tf_op jit(solution)/shard_map/ppermute | solution.py:29
  121.9 1.1 constant_dynamic-update-slice_fusion.11
  124.0 20.4 %collective-permute-done.13 = bf16[512,1024]{1,0:T(8,128)(2,1)S(1)} collective-permute-done((bf16[512,1024]{1,0:T(8,128)(2,1)S(1)}, bf16[512,1024]{1,0:T(8,128)(2,1)S(1)}, u32[]{:S(2)}, u32[]{:S(2)}) %collective-permute-start.13) | collective-permute-done | bytes 1048608 | tf_op jit(solution)/shard_map/ppermute | solution.py:29
  144.4 1.1 constant_dynamic-update-slice_fusion.8
  147.8 8.4 %fusion = f32[640,512]{1,0:T(8,128)} fusion(bf16[640,4096]{1,0:T(8,128)(2,1)S(1)} %constant_dynamic-update-slice_fusion.10, bf16[4096,1024]{1,0:T(8,128)(2,1)} %constant_dynamic-update-slice_fusion.6), kind=kOutput, calls=%fused_computation | convolution fusion | flops 2684354560 | bytes 10747904 | tf_op jit(solution)/shard_map/dot_general | solution.py:96
  156.2 4.5 %collective-permute-start.24 = (f32[640,512]{1,0:T(8,128)}, f32[640,512]{1,0:T(8,128)S(1)}, u32[]{:S(2)}, u32[]{:S(2)}) collective-permute-start(f32[640,512]{1,0:T(8,128)} %fusion), channel_id=1, source_target_pairs={{0,2},{2,0},{1,3},{3,1},{4,6},{6,4},{5,7},{7,5},{8,10},{10,8},{9,1... | collective-permute-start | bytes 3932168 | tf_op jit(solution)/shard_map/ppermute | solution.py:99
  160.8 8.0 %fusion.2 = f32[640,512]{1,0:T(8,128)} fusion(bf16[640,4096]{1,0:T(8,128)(2,1)S(1)} %constant_dynamic-update-slice_fusion.15, bf16[4096,1024]{1,0:T(8,128)(2,1)} %constant_dynamic-update-slice_fusion.6), kind=kOutput, calls=%fused_computation.2 | convolution fusion | flops 2684354560 | bytes 10747904 | tf_op jit(solution)/shard_map/dot_general | solution.py:96
  168.8 6.8 %fusion.14 = bf16[640,512]{1,0:T(8,128)(2,1)S(1)} fusion(f32[640,512]{1,0:T(8,128)S(1)} %collective-permute-done.24, bf16[640,4096]{1,0:T(8,128)(2,1)} %copy-done.1, bf16[4096,1024]{1,0:T(8,128)(2,1)} %constant_dynamic-update-slice_fusion.6), kind=kOutput, calls=%fused_computation.10 | convolution fusion | flops 2685009920 | bytes 11403264 | tf_op jit(solution)/shard_map/dot_general | solution.py:96
  175.6 5.4 %broadcast_select_fusion.1 = (bf16[640,512]{1,0:T(8,128)(2,1)S(1)}, bf16[640,512]{1,0:T(8,128)(2,1)S(1)}) fusion(bf16[640,512]{1,0:T(8,128)(2,1)S(1)} %fusion.14, pred[]{:T(512)S(6)} %eq.21, f32[640,512]{1,0:T(8,128)} %collective-permute-done.16, bf16[640,4096]{1,0:T(8,128)(2,1)S(1)} %bitcast.7, bf16[4096,1024]{1,0:T(8,128)(2,1)} %constant_dynamic-update-slice_fusion.6), kind=kOutput, calls=%fused_computation.17 | convolution fusion | flops 2685665280 | bytes 12713985 | tf_op jit(solution)/shard_map/dot_general | solution.py:96
  181.1 1.1 pad_maximum_fusion
  (63 shorter events, 10.4 us)
Async XLA Ops:
  1.3 28.9 %collective-permute-start.7 = (bf16[512,1024]{1,0:T(8,128)(2,1)S(1)}, bf16[512,1024]{1,0:T(8,128)(2,1)}, u32[]{:S(2)}, u32[]{:S(2)}) collective-permute-start(bf16[512,1024]{1,0:T(8,128)(2,1)S(1)} %constant_dynamic-slice_fusion.3), channel_id=1, source_target_pairs={{0,2},{2,0},{1,3},{3,1},{4,6},{6,4},{5,7},{7,5},{8,10},{10,8},{9,1... | collective-permute-start | bytes 3145736 | tf_op jit(solution)/shard_map/ppermute | solution.py:45
  6.0 19.1 %collective-permute-start = (bf16[640,512]{1,0:T(8,128)(2,1)S(1)}, bf16[640,512]{1,0:T(8,128)(2,1)}, u32[]{:S(2)}, u32[]{:S(2)}) collective-permute-start(bf16[640,512]{1,0:T(8,128)(2,1)S(1)} %get-tuple-element.7), channel_id=1, source_target_pairs={{0,4},{4,8},{8,12},{12,16},{16,20},{20,24},{24,28},{28,0},{1,5},{5... | collective-permute-start | bytes 1966088 | tf_op jit(solution)/shard_map/ppermute | solution.py:23
  6.0 19.0 %collective-permute-start.1 = (bf16[640,512]{1,0:T(8,128)(2,1)S(1)}, bf16[640,512]{1,0:T(8,128)(2,1)}, u32[]{:S(2)}, u32[]{:S(2)}) collective-permute-start(bf16[640,512]{1,0:T(8,128)(2,1)S(1)} %get-tuple-element.7), channel_id=1, source_target_pairs={{0,28},{4,0},{8,4},{12,8},{16,12},{20,16},{24,20},{28,24},{1,29},{... | collective-permute-start | bytes 1966088 | tf_op jit(solution)/shard_map/ppermute | solution.py:26
  25.1 17.2 %collective-permute-start.2 = (bf16[640,512]{1,0:T(8,128)(2,1)}, bf16[640,512]{1,0:T(8,128)(2,1)}, u32[]{:S(2)}, u32[]{:S(2)}) collective-permute-start(bf16[640,512]{1,0:T(8,128)(2,1)} %collective-permute-done), channel_id=1, source_target_pairs={{0,4},{4,8},{8,12},{12,16},{16,20},{20,24},{24,28},{28,0},{1,5},{5... | collective-permute-start | bytes 1966088 | tf_op jit(solution)/shard_map/ppermute | solution.py:23
  25.1 20.0 %collective-permute-start.3 = (bf16[640,512]{1,0:T(8,128)(2,1)}, bf16[640,512]{1,0:T(8,128)(2,1)}, u32[]{:S(2)}, u32[]{:S(2)}) collective-permute-start(bf16[640,512]{1,0:T(8,128)(2,1)} %collective-permute-done.1), channel_id=1, source_target_pairs={{0,28},{4,0},{8,4},{12,8},{16,12},{20,16},{24,20},{28,24},{1,29},{... | collective-permute-start | bytes 1966088 | tf_op jit(solution)/shard_map/ppermute | solution.py:26
  31.3 13.7 %collective-permute-start.12 = (bf16[256,1024]{1,0:T(8,128)(2,1)S(1)}, bf16[256,1024]{1,0:T(8,128)(2,1)}, u32[]{:S(2)}, u32[]{:S(2)}) collective-permute-start(bf16[256,1024]{1,0:T(8,128)(2,1)S(1)} %pad_maximum_fusion.2), channel_id=1, source_target_pairs={{32,1},{1,32},{33,0},{0,33},{34,3},{3,34},{35,2},{2,35},{36,5},{5,... | collective-permute-start | bytes 1572872 | tf_op jit(solution)/shard_map/ppermute | solution.py:57
  35.0 18.7 %collective-permute-start.11 = (bf16[256,1024]{1,0:T(8,128)(2,1)S(1)}, bf16[256,1024]{1,0:T(8,128)(2,1)}, u32[]{:S(2)}, u32[]{:S(2)}) collective-permute-start(bf16[256,1024]{1,0:T(8,128)(2,1)S(1)} %fusion.20), channel_id=1, source_target_pairs={{0,32},{32,0},{1,33},{33,1},{2,34},{34,2},{3,35},{35,3},{4,36},{36... | collective-permute-start | bytes 1572872 | tf_op jit(solution)/shard_map/ppermute | solution.py:56
  35.1 26.0 %collective-permute-start.17 = (bf16[640,512]{1,0:T(8,128)(2,1)}, bf16[640,512]{1,0:T(8,128)(2,1)S(1)}, u32[]{:S(2)}, u32[]{:S(2)}) collective-permute-start(bf16[640,512]{1,0:T(8,128)(2,1)} %collective-permute-done.1), channel_id=1, source_target_pairs={{0,1},{1,0},{2,3},{3,2},{4,5},{5,4},{6,7},{7,6},{8,9},{9,8},{10,11... | collective-permute-start | bytes 1966088 | tf_op jit(solution)/shard_map/ppermute | solution.py:35
  42.3 33.0 %collective-permute-start.18 = (bf16[640,512]{1,0:T(8,128)(2,1)}, bf16[640,512]{1,0:T(8,128)(2,1)}, u32[]{:S(2)}, u32[]{:S(2)}) collective-permute-start(bf16[640,512]{1,0:T(8,128)(2,1)} %collective-permute-done), channel_id=1, source_target_pairs={{0,1},{1,0},{2,3},{3,2},{4,5},{5,4},{6,7},{7,6},{8,9},{9,8},{10,11... | collective-permute-start | bytes 1966088 | tf_op jit(solution)/shard_map/ppermute | solution.py:35
  45.1 39.0 %collective-permute-start.4 = (bf16[640,512]{1,0:T(8,128)(2,1)}, bf16[640,512]{1,0:T(8,128)(2,1)}, u32[]{:S(2)}, u32[]{:S(2)}) collective-permute-start(bf16[640,512]{1,0:T(8,128)(2,1)} %collective-permute-done.2), channel_id=1, source_target_pairs={{0,4},{4,8},{8,12},{12,16},{16,20},{20,24},{24,28},{28,0},{1,5},{5... | collective-permute-start | bytes 1966088 | tf_op jit(solution)/shard_map/ppermute | solution.py:23
  45.1 41.0 %collective-permute-start.5 = (bf16[640,512]{1,0:T(8,128)(2,1)}, bf16[640,512]{1,0:T(8,128)(2,1)}, u32[]{:S(2)}, u32[]{:S(2)}) collective-permute-start(bf16[640,512]{1,0:T(8,128)(2,1)} %collective-permute-done.3), channel_id=1, source_target_pairs={{0,28},{4,0},{8,4},{12,8},{16,12},{20,16},{24,20},{28,24},{1,29},{... | collective-permute-start | bytes 1966088 | tf_op jit(solution)/shard_map/ppermute | solution.py:26
  53.7 45.7 %collective-permute-start.8 = (bf16[512,1024]{1,0:T(8,128)(2,1)}, bf16[512,1024]{1,0:T(8,128)(2,1)}, u32[]{:S(2)}, u32[]{:S(2)}) collective-permute-start(bf16[512,1024]{1,0:T(8,128)(2,1)} %get-tuple-element.9), channel_id=1, source_target_pairs={{0,64},{64,128},{128,192},{192,0},{1,65},{65,129},{129,193},{193,1... | collective-permute-start | bytes 3145736 | tf_op jit(solution)/shard_map/ppermute | solution.py:29
  61.1 2.7 %copy-start.3 = (bf16[640,512]{1,0:T(8,128)(2,1)}, bf16[640,512]{1,0:T(8,128)(2,1)S(1)}, u32[]{:S(2)}) copy-start(bf16[640,512]{1,0:T(8,128)(2,1)S(1)} %collective-permute-done.17) | copy-start | bytes 1966084
  61.1 41.3 %collective-permute-start.9 = (bf16[512,1024]{1,0:T(8,128)(2,1)}, bf16[512,1024]{1,0:T(8,128)(2,1)}, u32[]{:S(2)}, u32[]{:S(2)}) collective-permute-start(bf16[512,1024]{1,0:T(8,128)(2,1)} %get-tuple-element.9), channel_id=1, source_target_pairs={{0,192},{64,0},{128,64},{192,128},{1,193},{65,1},{129,65},{193,129... | collective-permute-start | bytes 3145736 | tf_op jit(solution)/shard_map/ppermute | solution.py:32
  75.3 29.6 %collective-permute-start.14 = (bf16[512,1024]{1,0:T(8,128)(2,1)S(1)}, bf16[512,1024]{1,0:T(8,128)(2,1)S(1)}, u32[]{:S(2)}, u32[]{:S(2)}) collective-permute-start(bf16[512,1024]{1,0:T(8,128)(2,1)S(1)} %constant_dynamic-update-slice_fusion.22), channel_id=1, source_target_pairs={{0,192},{64,0},{128,64},{192,128},{1,193},{65,1},{129,65},{193,129... | collective-permute-start | bytes 3145736 | tf_op jit(solution)/shard_map/ppermute | solution.py:32
  81.0 3.0 %copy-start.4 = (bf16[640,512]{1,0:T(8,128)(2,1)S(1)}, bf16[640,512]{1,0:T(8,128)(2,1)}, u32[]{:S(2)}) copy-start(bf16[640,512]{1,0:T(8,128)(2,1)} %copy-done.3) | copy-start | bytes 1966084
  84.0 13.7 %collective-permute-start.19 = (bf16[640,512]{1,0:T(8,128)(2,1)S(1)}, bf16[640,512]{1,0:T(8,128)(2,1)S(1)}, u32[]{:S(2)}, u32[]{:S(2)}) collective-permute-start(bf16[640,512]{1,0:T(8,128)(2,1)S(1)} %copy-done.4), channel_id=1, source_target_pairs={{0,28},{4,0},{8,4},{12,8},{16,12},{20,16},{24,20},{28,24},{1,29},{... | collective-permute-start | bytes 1966088 | tf_op jit(solution)/shard_map/ppermute | solution.py:26
  86.0 15.5 %collective-permute-start.21 = (bf16[640,512]{1,0:T(8,128)(2,1)}, bf16[640,512]{1,0:T(8,128)(2,1)S(1)}, u32[]{:S(2)}, u32[]{:S(2)}) collective-permute-start(bf16[640,512]{1,0:T(8,128)(2,1)} %collective-permute-done.18), channel_id=1, source_target_pairs={{0,4},{4,8},{8,12},{12,16},{16,20},{20,24},{24,28},{28,0},{1,5},{5... | collective-permute-start | bytes 1966088 | tf_op jit(solution)/shard_map/ppermute | solution.py:23
  97.7 14.6 %collective-permute-start.20 = (bf16[640,512]{1,0:T(8,128)(2,1)}, bf16[640,512]{1,0:T(8,128)(2,1)S(1)}, u32[]{:S(2)}, u32[]{:S(2)}) collective-permute-start(bf16[640,512]{1,0:T(8,128)(2,1)} %collective-permute-done.4), channel_id=1, source_target_pairs={{0,1},{1,0},{2,3},{3,2},{4,5},{5,4},{6,7},{7,6},{8,9},{9,8},{10,11... | collective-permute-start | bytes 1966088 | tf_op jit(solution)/shard_map/ppermute | solution.py:35
  99.4 22.5 %collective-permute-start.10 = (bf16[512,1024]{1,0:T(8,128)(2,1)}, bf16[512,1024]{1,0:T(8,128)(2,1)S(1)}, u32[]{:S(2)}, u32[]{:S(2)}) collective-permute-start(bf16[512,1024]{1,0:T(8,128)(2,1)} %collective-permute-done.8), channel_id=1, source_target_pairs={{0,64},{64,128},{128,192},{192,0},{1,65},{65,129},{129,193},{193,1... | collective-permute-start | bytes 3145736 | tf_op jit(solution)/shard_map/ppermute | solution.py:29
  101.5 14.1 %collective-permute-start.6 = (bf16[640,512]{1,0:T(8,128)(2,1)}, bf16[640,512]{1,0:T(8,128)(2,1)S(1)}, u32[]{:S(2)}, u32[]{:S(2)}) collective-permute-start(bf16[640,512]{1,0:T(8,128)(2,1)} %collective-permute-done.4), channel_id=1, source_target_pairs={{0,4},{4,8},{8,12},{12,16},{16,20},{20,24},{24,28},{28,0},{1,5},{5... | collective-permute-start | bytes 1966088 | tf_op jit(solution)/shard_map/ppermute | solution.py:23
  102.4 12.5 %copy-start = (bf16[640,4096]{1,0:T(8,128)(2,1)S(1)}, bf16[640,4096]{1,0:T(8,128)(2,1)}, u32[]{:S(2)}) copy-start(bf16[640,4096]{1,0:T(8,128)(2,1)} %constant_dynamic-update-slice_fusion.3) | copy-start | bytes 15728644
  102.4 42.0 %collective-permute-start.13 = (bf16[512,1024]{1,0:T(8,128)(2,1)S(1)}, bf16[512,1024]{1,0:T(8,128)(2,1)S(1)}, u32[]{:S(2)}, u32[]{:S(2)}) collective-permute-start(bf16[512,1024]{1,0:T(8,128)(2,1)S(1)} %constant_dynamic-update-slice_fusion.22), channel_id=1, source_target_pairs={{0,64},{64,128},{128,192},{192,0},{1,65},{65,129},{129,193},{193,1... | collective-permute-start | bytes 3145736 | tf_op jit(solution)/shard_map/ppermute | solution.py:29
  104.9 12.3 %collective-permute-start.22 = (bf16[640,512]{1,0:T(8,128)(2,1)S(1)}, bf16[640,512]{1,0:T(8,128)(2,1)S(1)}, u32[]{:S(2)}, u32[]{:S(2)}) collective-permute-start(bf16[640,512]{1,0:T(8,128)(2,1)S(1)} %collective-permute-done.19), channel_id=1, source_target_pairs={{0,28},{4,0},{8,4},{12,8},{16,12},{20,16},{24,20},{28,24},{1,29},{... | collective-permute-start | bytes 1966088 | tf_op jit(solution)/shard_map/ppermute | solution.py:26
  112.3 34.4 %collective-permute-start.15 = (bf16[512,1024]{1,0:T(8,128)(2,1)S(1)}, bf16[512,1024]{1,0:T(8,128)(2,1)S(1)}, u32[]{:S(2)}, u32[]{:S(2)}) collective-permute-start(bf16[512,1024]{1,0:T(8,128)(2,1)S(1)} %collective-permute-done.14), channel_id=1, source_target_pairs={{0,192},{64,0},{128,64},{192,128},{1,193},{65,1},{129,65},{193,129... | collective-permute-start | bytes 3145736 | tf_op jit(solution)/shard_map/ppermute | solution.py:32
  115.6 31.0 %collective-permute-start.23 = (bf16[640,512]{1,0:T(8,128)(2,1)S(1)}, bf16[640,512]{1,0:T(8,128)(2,1)S(1)}, u32[]{:S(2)}, u32[]{:S(2)}) collective-permute-start(bf16[640,512]{1,0:T(8,128)(2,1)S(1)} %collective-permute-done.6), channel_id=1, source_target_pairs={{0,1},{1,0},{2,3},{3,2},{4,5},{5,4},{6,7},{7,6},{8,9},{9,8},{10,11... | collective-permute-start | bytes 1966088 | tf_op jit(solution)/shard_map/ppermute | solution.py:35
  146.7 9.5 %copy-start.1 = (bf16[640,4096]{1,0:T(8,128)(2,1)}, bf16[640,4096]{1,0:T(8,128)(2,1)S(1)}, u32[]{:S(2)}) copy-start(bf16[640,4096]{1,0:T(8,128)(2,1)S(1)} %constant_dynamic-update-slice_fusion.10) | copy-start | bytes 15728644
  146.7 14.0 %slice-start = ((s8[5242880]{0:T(1024)(128)(4,1)}), s8[4194304]{0:T(1024)(128)(4,1)S(1)}, s32[]{:S(2)}) async-start(s8[5242880]{0:T(1024)(128)(4,1)} %bitcast.4), calls=%async_computation | async-start | bytes 8388608
  147.8 12.9 %slice-start.1 = ((s8[5242880]{0:T(1024)(128)(4,1)}), s8[1048576]{0:T(1024)(128)(4,1)S(1)}, s32[]{:S(2)}) async-start(s8[5242880]{0:T(1024)(128)(4,1)} %bitcast.4), calls=%async_computation.1 | async-start | bytes 2097152
  156.2 12.6 %collective-permute-start.24 = (f32[640,512]{1,0:T(8,128)}, f32[640,512]{1,0:T(8,128)S(1)}, u32[]{:S(2)}, u32[]{:S(2)}) collective-permute-start(f32[640,512]{1,0:T(8,128)} %fusion), channel_id=1, source_target_pairs={{0,2},{2,0},{1,3},{3,1},{4,6},{6,4},{5,7},{7,5},{8,10},{10,8},{9,1... | collective-permute-start | bytes 3932168 | tf_op jit(solution)/shard_map/ppermute | solution.py:99
  160.8 8.0 %copy-start.2 = (bf16[640,4096]{1,0:T(8,128)(2,1)}, bf16[640,4096]{1,0:T(8,128)(2,1)S(1)}, u32[]{:S(2)}) copy-start(bf16[640,4096]{1,0:T(8,128)(2,1)S(1)} %constant_dynamic-update-slice_fusion.15) | copy-start | bytes 15728644
  168.8 6.8 %collective-permute-start.16 = (f32[640,512]{1,0:T(8,128)}, f32[640,512]{1,0:T(8,128)}, u32[]{:S(2)}, u32[]{:S(2)}) collective-permute-start(f32[640,512]{1,0:T(8,128)} %fusion.2), channel_id=1, source_target_pairs={{0,2},{2,0},{1,3},{3,1},{4,6},{6,4},{5,7},{7,5},{8,10},{10,8},{9,1... | collective-permute-start | bytes 3932168 | tf_op jit(solution)/shard_map/ppermute | solution.py:98
  168.8 6.8 %slice-start.2 = ((s8[5242880]{0:T(1024)(128)(4,1)}), s8[1048576]{0:T(1024)(128)(4,1)S(1)}, s32[]{:S(2)}) async-start(s8[5242880]{0:T(1024)(128)(4,1)} %bitcast.6), calls=%async_computation.2 | async-start | bytes 2097152
  168.8 6.8 %slice-start.3 = ((s8[5242880]{0:T(1024)(128)(4,1)}), s8[4194304]{0:T(1024)(128)(4,1)S(1)}, s32[]{:S(2)}) async-start(s8[5242880]{0:T(1024)(128)(4,1)} %bitcast.6), calls=%async_computation.3 | async-start | bytes 8388608

commit v2 on v0

v2 whole, which is shorter than its diff:
```python
import jax
import jax.numpy as jnp
from jax import lax
from jax.experimental import pallas as pl
from jax.experimental.pallas import tpu as pltpu
from jax.sharding import Mesh
from jax.sharding import PartitionSpec as P


AXES = ("y", "xl", "z", "core", "xh")
ROWS = 256


def ring(size, shift):
    return [(i, (i + shift) % size) for i in range(size)]


def product_kernel(counts, *refs):
    zn, yn, na, nb = counts
    a_refs, b_refs, c_refs = refs[:zn], refs[zn : 2 * zn], refs[2 * zn : 3 * zn]
    w_refs = refs[3 * zn : 4 * zn]
    out_ref, t_buf, w_buf, acc, sem, out_sem = refs[4 * zn :]
    y, xl, z, xh = (lax.axis_index(name) for name in ("y", "xl", "z", "xh"))
    width = w_buf.shape[2]

    def token_copies(d, slot):
        at = pl.multiple_of(xh * nb, nb)
        other = pl.multiple_of((1 - xh) * nb, nb)
        return (
            pltpu.make_async_copy(
                a_refs[d], t_buf.at[slot, pl.ds(2 * nb, na)], sem.at[slot, 0]
            ),
            pltpu.make_async_copy(b_refs[d], t_buf.at[slot, pl.ds(at, nb)], sem.at[slot, 1]),
            pltpu.make_async_copy(c_refs[d], t_buf.at[slot, pl.ds(other, nb)], sem.at[slot, 2]),
        )

    def weight_copy(index, slot):
        ref, column = w_refs[index]
        return pltpu.make_async_copy(
            ref.at[:, pl.ds(column, width)], w_buf.at[slot], sem.at[slot, 3]
        )

    def start(d, slot):
        for copy in token_copies(d, slot):
            copy.start()
        block = lax.rem(z + d, zn)
        across = lax.rem(block // 2 - y + yn, yn)
        side = lax.rem(block, 2)
        wanted = 2 * across + jnp.where(side == xl, 0, 1)
        for index in range(zn):
            @pl.when(wanted == index)
            def _():
                weight_copy(index, slot).start()

    def wait(d, slot):
        for copy in token_copies(d, slot):
            copy.wait()
        weight_copy(0, slot).wait()

    rows = t_buf.shape[1]
    steps = rows // ROWS
    start(0, 0)
    for d in range(zn):
        slot = d % 2
        if d + 1 < zn:
            start(d + 1, 1 - slot)
        wait(d, slot)

        def tile(i, carry):
            at = pl.ds(pl.multiple_of(i * ROWS, ROWS), ROWS)
            part = jnp.dot(
                t_buf[slot, at, :], w_buf[slot], preferred_element_type=jnp.float32
            )
            acc[at, :] = part if d == 0 else acc[at, :] + part
            return carry

        lax.fori_loop(0, steps, tile, 0)
    out = pltpu.make_async_copy(acc, out_ref, out_sem)
    out.start()
    out.wait()


def block_product(counts, a, b, c, weights, columns):
    zn, _, na, nb = counts
    rows, depth = na + 2 * nb, a[0].shape[1]
    width = 512

    def kernel(*refs):
        w = [(ref, at) for ref, at in zip(refs[3 * zn : 4 * zn], columns)]
        product_kernel(counts, *refs[: 3 * zn], *w, *refs[4 * zn :])

    anywhere = pl.BlockSpec(memory_space=pl.ANY)
    return pl.pallas_call(
        kernel,
        out_shape=jax.ShapeDtypeStruct((rows, width), jnp.float32),
        in_specs=[anywhere] * (4 * zn),
        out_specs=anywhere,
        scratch_shapes=[
            pltpu.VMEM((2, rows, depth), jnp.bfloat16),
            pltpu.VMEM((2, depth, width), jnp.bfloat16),
            pltpu.VMEM((rows, width), jnp.float32),
            pltpu.SemaphoreType.DMA((2, 4)),
            pltpu.SemaphoreType.DMA,
        ],
        compiler_params=pltpu.CompilerParams(vmem_limit_bytes=16 * 1024 * 1024),
        cost_estimate=pl.CostEstimate(
            flops=2 * rows * width * depth * zn,
            bytes_accessed=2 * zn * depth * (rows + width) + 4 * rows * width,
            transcendentals=0,
        ),
    )(*a, *b, *c, *weights)


def per_device(tokens, up_weight):
    core, xh = lax.axis_index("core"), lax.axis_index("xh")
    zn, yn = lax.axis_size("z"), lax.axis_size("y")
    rows, depth = tokens.shape
    nb = 3 * rows // 10
    na = rows - 2 * nb
    width = up_weight.shape[1] // 2

    def up(axis, a):
        return lax.ppermute(a, axis, ring(lax.axis_size(axis), 1))

    def down(axis, a):
        return lax.ppermute(a, axis, ring(lax.axis_size(axis), -1))

    def crossed(a, shift):
        pairs = [
            (2 * i + k, 2 * ((i + shift) % yn) + 1 - k) for i in range(yn) for k in range(2)
        ]
        return lax.ppermute(a, ("y", "core"), pairs)

    def quarter(parity, layer):
        return lax.dynamic_slice(
            up_weight, (parity * depth, layer * width), (depth, width)
        )

    b, c, a = {}, {}, {}
    b[0] = lax.dynamic_slice_in_dim(tokens, xh * nb, nb, 0)
    c[0] = lax.dynamic_slice_in_dim(tokens, (1 - xh) * nb, nb, 0)
    a[0] = tokens[2 * nb :]
    mine, given, far = quarter(core, xh), quarter(1 - core, xh), quarter(1 - core, 1 - xh)

    b[-1], b[1] = up("z", b[0]), down("z", b[0])
    a[-1], a[1] = up("z", a[0]), down("z", a[0])
    b[-2], b[2] = up("z", b[-1]), down("z", b[1])
    a[-2], a[2] = up("z", a[-1]), down("z", a[1])
    b[-3], b[3] = up("z", b[-2]), down("z", b[2])
    a[-3], a[3] = up("z", a[-2]), down("z", a[2])
    b[4], a[4] = down("z", b[3]), up("z", a[-3])
    for d in (-1, 1, -2, 2, -3, 3, 4):
        c[d] = lax.ppermute(b[d], "xh", ring(2, 1))

    wa, wb, wo = {0: mine}, {}, {}
    wa[-1], wa[1] = up("y", mine), down("y", mine)
    wb[-1], wb[1] = crossed(given, 1), crossed(given, -1)
    near = lax.ppermute(mine, "xl", ring(2, 1))
    across = lax.ppermute(far, ("xl", "core", "xh"), [(i, 7 - i) for i in range(8)])
    wb[0] = lax.ppermute(given, "core", ring(2, 1))
    wo[0] = jnp.concatenate([near, across], 1)
    wo[-1], wo[1] = up("y", wo[0]), down("y", wo[0])
    wa[2], wb[2] = up("y", wa[-1]), up("y", wb[-1])
    wo[2] = down("y", wo[1])

    def turn(pieces, size):
        return [pieces[d if d in pieces else d - size] for d in range(size)]

    counts = (zn, yn, na, nb)
    tokens_in = [turn(t, zn) for t in (a, b, c)]
    wa, wb, wo = (turn(w, yn) for w in (wa, wb, wo))

    def mixed(first):
        return [w for pair in zip(first, wo) for w in pair]

    partner = block_product(counts, *tokens_in, mixed(wb), (0, width) * yn)
    swapped = lax.ppermute(partner, "core", ring(2, 1))
    own = block_product(counts, *tokens_in, mixed(wa), (0, 0) * yn)
    return (own + swapped).astype(jnp.bfloat16)


def solution(mesh):
    split = Mesh(
        mesh.devices.reshape(4, 2, mesh.shape["col"] // 2, 2, mesh.shape["layer"]), AXES
    )
    spec = P(("y", "xl"), ("z", "core"))
    return jax.shard_map(
        per_device,
        mesh=split,
        in_specs=(spec, spec),
        out_specs=P(("y", "xl"), ("z", "core", "xh")),
        check_vma=False,
    )
```

time: 283 us -> 183 us (0.65)
  waiting for transfers between devices: 249 us -> 82.2 us
  starting transfers between devices: 0.08 us -> 61 us
  Pallas kernels: 0 us -> 34.1 us
  matrix products: 16.7 us -> 0 us
  between operations: 13.1 us -> 0.1 us
    all_gather x3 -> x0, waiting for transfers between devices: 248 us -> none  [the longest x2 130 us: gather_axes(): result = lax.all_gather(result, axes[number], axis=dim, tiled=True)]
    ppermute x0 -> x34, waiting for transfers between devices: none -> 82.2 us  [the longest x11 45.3 us: up(): return lax.ppermute(a, axis, ring(lax.axis_size(axis), 1))]
    ppermute x0 -> x34, starting transfers between devices: none -> 61 us  [the longest x10 22.7 us: down(): return lax.ppermute(a, axis, ring(lax.axis_size(axis), -1))]
    pallas_call x0 -> x2, Pallas kernels: none -> 34.1 us  [block_product(): pl.pallas_call(kernel, out_shape=jax.ShapeDtypeStruct((rows, width), jnp....]
    dot_general x1 -> x0, matrix products: 16.7 us -> none  [per_device(): jnp.dot(token_whole, gather_axes(weight_part, ROW, 0), preferred_element_...]
  transfers between devices with their start and end apart: 3 -> 34, of which waited for: 3 -> 14; matrix products, arithmetic and copies ran while one was open for 0% -> 1% of each run, Pallas kernels for 0% -> 9%
where the time goes in v2:
time: 183 us
  waiting for transfers between devices  82.2 us (45%)
  starting transfers between devices  61 us (33%)
  Pallas kernels  34.1 us (19%)
  local copies, waits for them, and re-layouts  3.84 us (2%)
    ppermute x11, waiting for transfers between devices, up(): return lax.ppermute(a, axis, ring(lax.axis_size(axis), 1))  45.3 us
    pallas_call x2, Pallas kernels, block_product(): pl.pallas_call(kernel, out_shape=jax.ShapeDtypeStruct((rows, width), jnp....  34.1 us
    ppermute x10, starting transfers between devices, down(): return lax.ppermute(a, axis, ring(lax.axis_size(axis), -1))  22.7 us
    ppermute x10, waiting for transfers between devices, down(): return lax.ppermute(a, axis, ring(lax.axis_size(axis), -1))  15.2 us
    ppermute x7, waiting for transfers between devices, per_device(): c[d] = lax.ppermute(b[d], 'xh', ring(2, 1))  15.2 us
    ppermute x7, starting transfers between devices, per_device(): c[d] = lax.ppermute(b[d], 'xh', ring(2, 1))  14.6 us
    ppermute x1, starting transfers between devices, per_device(): swapped = lax.ppermute(partner, 'core', ring(2, 1))  7.39 us
    ppermute x2, starting transfers between devices, crossed(): return lax.ppermute(a, ('y', 'core'), pairs)  6.62 us
  transfers between devices with their start and end apart: 34, of which 14 were waited for; matrix products, arithmetic and copies ran while one was open for 1% of the time, Pallas kernels for 9%

profile of v2, /device:TPU:1, one launch (start us, length us, event | category | flops | bytes accessed | tf_op | source)
XLA Modules:
  0.0 182.7 jit_solution(9604665340224722430)
XLA Ops:
  0.0 1.2 constant_dynamic-slice_fusion
  1.2 2.5 %collective-permute-start.11 = (bf16[384,512]{1,0:T(8,128)(2,1)S(1)}, bf16[384,512]{1,0:T(8,128)(2,1)S(1)}, u32[]{:S(2)}, u32[]{:S(2)}) collective-permute-start(bf16[384,512]{1,0:T(8,128)(2,1)S(1)} %get-tuple-element.9.refs_8_), channel_id=1, source_target_pairs={{0,4},{4,8},{8,12},{12,16},{16,20},{20,24},{24,28},{28,0},{1,5},{5... | collective-permute-start | bytes 1179656 | tf_op jit(solution)/shard_map/ppermute | solution.py:123
  3.7 4.0 %collective-permute-start.7 = (bf16[384,512]{1,0:T(8,128)(2,1)S(1)}, bf16[384,512]{1,0:T(8,128)(2,1)S(1)}, u32[]{:S(2)}, u32[]{:S(2)}) collective-permute-start(bf16[384,512]{1,0:T(8,128)(2,1)S(1)} %get-tuple-element.9.refs_8_), channel_id=1, source_target_pairs={{0,28},{4,0},{8,4},{12,8},{16,12},{20,16},{24,20},{28,24},{1,29},{... | collective-permute-start | bytes 1179656 | tf_op jit(solution)/shard_map/ppermute | solution.py:126
  7.7 1.1 slice.3.refs_0_
  8.8 0.1 collective-permute-start.3
  8.9 2.7 %collective-permute-start = (bf16[512,512]{1,0:T(8,128)(2,1)S(1)}, bf16[512,512]{1,0:T(8,128)(2,1)S(1)}, u32[]{:S(2)}, u32[]{:S(2)}) collective-permute-start(bf16[512,512]{1,0:T(8,128)(2,1)S(1)} %slice.3.refs_0_), channel_id=1, source_target_pairs={{0,28},{4,0},{8,4},{12,8},{16,12},{20,16},{24,20},{28,24},{1,29},{... | collective-permute-start | bytes 1572872 | tf_op jit(solution)/shard_map/ppermute | solution.py:126
  11.6 1.5 fusion
  13.0 4.0 %collective-permute-start.22 = (bf16[512,512]{1,0:T(8,128)(2,1)S(1)}, bf16[512,512]{1,0:T(8,128)(2,1)S(1)}, u32[]{:S(2)}, u32[]{:S(2)}) collective-permute-start(bf16[512,512]{1,0:T(8,128)(2,1)S(1)} %get-tuple-element.7), channel_id=1, source_target_pairs={{0,35},{1,34},{2,33},{3,32},{32,3},{33,2},{34,1},{35,0},{4,39},{5,... | collective-permute-start | bytes 1572872 | tf_op jit(solution)/shard_map/ppermute | solution.py:159
  17.0 2.7 %collective-permute-start.31 = (bf16[512,512]{1,0:T(8,128)(2,1)S(1)}, bf16[512,512]{1,0:T(8,128)(2,1)S(1)}, u32[]{:S(2)}, u32[]{:S(2)}) collective-permute-start(bf16[512,512]{1,0:T(8,128)(2,1)S(1)} %get-tuple-element.5), channel_id=1, source_target_pairs={{0,66},{2,64},{64,130},{66,128},{128,194},{130,192},{192,2},{194,0... | collective-permute-start | bytes 1572872 | tf_op jit(solution)/shard_map/ppermute | solution.py:132
  19.7 1.2 collective-permute-start.21
  21.0 6.7 %collective-permute-done.3.refs_7_ = bf16[512,512]{1,0:T(8,128)(2,1)S(1)} collective-permute-done((bf16[512,512]{1,0:T(8,128)(2,1)S(1)}, bf16[512,512]{1,0:T(8,128)(2,1)S(1)}, u32[]{:S(2)}, u32[]{:S(2)}) %collective-permute-start.3) | collective-permute-done | bytes 524320 | tf_op jit(solution)/shard_map/ppermute | solution.py:123
  27.7 3.9 %collective-permute-start.30 = (bf16[512,512]{1,0:T(8,128)(2,1)S(1)}, bf16[512,512]{1,0:T(8,128)(2,1)S(1)}, u32[]{:S(2)}, u32[]{:S(2)}) collective-permute-start(bf16[512,512]{1,0:T(8,128)(2,1)S(1)} %get-tuple-element.5), channel_id=1, source_target_pairs={{0,194},{2,192},{64,2},{66,0},{128,66},{130,64},{192,130},{194,128... | collective-permute-start | bytes 1572872 | tf_op jit(solution)/shard_map/ppermute | solution.py:132
  31.6 2.8 %collective-permute-start.20 = (bf16[384,512]{1,0:T(8,128)(2,1)S(1)}, bf16[384,512]{1,0:T(8,128)(2,1)S(1)}, u32[]{:S(2)}, u32[]{:S(2)}) collective-permute-start(bf16[384,512]{1,0:T(8,128)(2,1)S(1)} %collective-permute-done.11.refs_15_), channel_id=1, source_target_pairs={{0,1},{1,0},{2,3},{3,2},{4,5},{5,4},{6,7},{7,6},{8,9},{9,8},{10,11... | collective-permute-start | bytes 1179656 | tf_op jit(solution)/shard_map/ppermute | solution.py:153
  34.4 1.6 collective-permute-start.14
  36.1 0.1 constant_dynamic-update-slice_fusion.refs_25_
  36.2 6.6 %collective-permute-done.30.refs_26_ = bf16[512,512]{1,0:T(8,128)(2,1)S(1)} collective-permute-done((bf16[512,512]{1,0:T(8,128)(2,1)S(1)}, bf16[512,512]{1,0:T(8,128)(2,1)S(1)}, u32[]{:S(2)}, u32[]{:S(2)}) %collective-permute-start.30) | collective-permute-done | bytes 524320 | tf_op jit(solution)/shard_map/ppermute | solution.py:132
  42.8 2.8 %collective-permute-start.24 = (bf16[512,1024]{1,0:T(8,128)(2,1)S(1)}, bf16[512,1024]{1,0:T(8,128)(2,1)S(1)}, u32[]{:S(2)}, u32[]{:S(2)}) collective-permute-start(bf16[512,1024]{1,0:T(8,128)(2,1)S(1)} %constant_dynamic-update-slice_fusion.refs_25_), channel_id=1, source_target_pairs={{0,192},{64,0},{128,64},{192,128},{1,193},{65,1},{129,65},{193,129... | collective-permute-start | bytes 3145736 | tf_op jit(solution)/shard_map/ppermute | solution.py:126
  45.6 0.9 collective-permute-start.8
  46.5 0.6 collective-permute-start.4
  47.1 2.1 %collective-permute-start.1 = (bf16[512,512]{1,0:T(8,128)(2,1)S(1)}, bf16[512,512]{1,0:T(8,128)(2,1)S(1)}, u32[]{:S(2)}, u32[]{:S(2)}) collective-permute-start(bf16[512,512]{1,0:T(8,128)(2,1)S(1)} %collective-permute-done.refs_1_), channel_id=1, source_target_pairs={{0,28},{4,0},{8,4},{12,8},{16,12},{20,16},{24,20},{28,24},{1,29},{... | collective-permute-start | bytes 1572872 | tf_op jit(solution)/shard_map/ppermute | solution.py:126
  49.2 2.7 %collective-permute-done.14.refs_17_ = bf16[384,512]{1,0:T(8,128)(2,1)S(1)} collective-permute-done((bf16[384,512]{1,0:T(8,128)(2,1)S(1)}, bf16[384,512]{1,0:T(8,128)(2,1)S(1)}, u32[]{:S(2)}, u32[]{:S(2)}) %collective-permute-start.14) | collective-permute-done | bytes 393248 | tf_op jit(solution)/shard_map/ppermute | solution.py:153
  51.8 1.2 collective-permute-start.32
  53.0 2.0 %collective-permute-done.8.refs_10_ = bf16[384,512]{1,0:T(8,128)(2,1)S(1)} collective-permute-done((bf16[384,512]{1,0:T(8,128)(2,1)S(1)}, bf16[384,512]{1,0:T(8,128)(2,1)S(1)}, u32[]{:S(2)}, u32[]{:S(2)}) %collective-permute-start.8) | collective-permute-done | bytes 393248 | tf_op jit(solution)/shard_map/ppermute | solution.py:126
  55.0 2.7 %collective-permute-start.19 = (bf16[384,512]{1,0:T(8,128)(2,1)S(1)}, bf16[384,512]{1,0:T(8,128)(2,1)S(1)}, u32[]{:S(2)}, u32[]{:S(2)}) collective-permute-start(bf16[384,512]{1,0:T(8,128)(2,1)S(1)} %collective-permute-done.12.refs_14_), channel_id=1, source_target_pairs={{0,1},{1,0},{2,3},{3,2},{4,5},{5,4},{6,7},{7,6},{8,9},{9,8},{10,11... | collective-permute-start | bytes 1179656 | tf_op jit(solution)/shard_map/ppermute | solution.py:153
  57.8 1.6 collective-permute-done.4.refs_6_
  59.4 0.2 collective-permute-start.28
  59.6 6.7 %collective-permute-done.1.refs_2_ = bf16[512,512]{1,0:T(8,128)(2,1)S(1)} collective-permute-done((bf16[512,512]{1,0:T(8,128)(2,1)S(1)}, bf16[512,512]{1,0:T(8,128)(2,1)S(1)}, u32[]{:S(2)}, u32[]{:S(2)}) %collective-permute-start.1) | collective-permute-done | bytes 524320 | tf_op jit(solution)/shard_map/ppermute | solution.py:126
  66.3 2.7 %collective-permute-start.15 = (bf16[384,512]{1,0:T(8,128)(2,1)S(1)}, bf16[384,512]{1,0:T(8,128)(2,1)S(1)}, u32[]{:S(2)}, u32[]{:S(2)}) collective-permute-start(bf16[384,512]{1,0:T(8,128)(2,1)S(1)} %collective-permute-done.8.refs_10_), channel_id=1, source_target_pairs={{0,1},{1,0},{2,3},{3,2},{4,5},{5,4},{6,7},{7,6},{8,9},{9,8},{10,11... | collective-permute-start | bytes 1179656 | tf_op jit(solution)/shard_map/ppermute | solution.py:153
  69.0 2.7 %collective-permute-start.9 = (bf16[384,512]{1,0:T(8,128)(2,1)S(1)}, bf16[384,512]{1,0:T(8,128)(2,1)S(1)}, u32[]{:S(2)}, u32[]{:S(2)}) collective-permute-start(bf16[384,512]{1,0:T(8,128)(2,1)S(1)} %collective-permute-done.8.refs_10_), channel_id=1, source_target_pairs={{0,28},{4,0},{8,4},{12,8},{16,12},{20,16},{24,20},{28,24},{1,29},{... | collective-permute-start | bytes 1179656 | tf_op jit(solution)/shard_map/ppermute | solution.py:126
  71.7 4.4 %collective-permute-done.13.refs_13_ = bf16[384,512]{1,0:T(8,128)(2,1)S(1)} collective-permute-done((bf16[384,512]{1,0:T(8,128)(2,1)S(1)}, bf16[384,512]{1,0:T(8,128)(2,1)S(1)}, u32[]{:S(2)}, u32[]{:S(2)}) %collective-permute-start.13) | collective-permute-done | bytes 393248 | tf_op jit(solution)/shard_map/ppermute | solution.py:123
  76.1 0.8 collective-permute-start.27
  76.9 2.7 %collective-permute-start.2 = (bf16[512,512]{1,0:T(8,128)(2,1)S(1)}, bf16[512,512]{1,0:T(8,128)(2,1)S(1)}, u32[]{:S(2)}, u32[]{:S(2)}) collective-permute-start(bf16[512,512]{1,0:T(8,128)(2,1)S(1)} %collective-permute-done.1.refs_2_), channel_id=1, source_target_pairs={{0,28},{4,0},{8,4},{12,8},{16,12},{20,16},{24,20},{28,24},{1,29},{... | collective-permute-start | bytes 1572872 | tf_op jit(solution)/shard_map/ppermute | solution.py:126
  79.6 1.4 collective-permute-start.10
  80.9 6.9 %collective-permute-done.5.refs_5_ = bf16[512,512]{1,0:T(8,128)(2,1)S(1)} collective-permute-done((bf16[512,512]{1,0:T(8,128)(2,1)S(1)}, bf16[512,512]{1,0:T(8,128)(2,1)S(1)}, u32[]{:S(2)}, u32[]{:S(2)}) %collective-permute-start.5) | collective-permute-done | bytes 524320 | tf_op jit(solution)/shard_map/ppermute | solution.py:123
  87.8 1.0 collective-permute-done.2.refs_3_
  88.8 1.7 collective-permute-start.16
  90.6 1.3 collective-permute-start.18
  91.8 5.5 %collective-permute-done.10.refs_12_ = bf16[384,512]{1,0:T(8,128)(2,1)S(1)} collective-permute-done((bf16[384,512]{1,0:T(8,128)(2,1)S(1)}, bf16[384,512]{1,0:T(8,128)(2,1)S(1)}, u32[]{:S(2)}, u32[]{:S(2)}) %collective-permute-start.10) | collective-permute-done | bytes 393248 | tf_op jit(solution)/shard_map/ppermute | solution.py:126
  97.3 1.6 collective-permute-start.17
  98.9 4.1 %collective-permute-done.18.refs_21_ = bf16[384,512]{1,0:T(8,128)(2,1)S(1)} collective-permute-done((bf16[384,512]{1,0:T(8,128)(2,1)S(1)}, bf16[384,512]{1,0:T(8,128)(2,1)S(1)}, u32[]{:S(2)}, u32[]{:S(2)}) %collective-permute-start.18) | collective-permute-done | bytes 393248 | tf_op jit(solution)/shard_map/ppermute | solution.py:153
  103.0 8.4 %collective-permute-done.17.refs_20_ = bf16[384,512]{1,0:T(8,128)(2,1)S(1)} collective-permute-done((bf16[384,512]{1,0:T(8,128)(2,1)S(1)}, bf16[384,512]{1,0:T(8,128)(2,1)S(1)}, u32[]{:S(2)}, u32[]{:S(2)}) %collective-permute-start.17) | collective-permute-done | bytes 393248 | tf_op jit(solution)/shard_map/ppermute | solution.py:153
  111.4 17.1 %shard_map.29 = f32[1280,512]{1,0:T(8,128)S(1)} custom-call(bf16[512,512]{1,0:T(8,128)(2,1)S(1)} %slice.3.refs_0_, bf16[512,512]{1,0:T(8,128)(2,1)S(1)} %collective-permute-done.refs_1_, bf16[512,512]{1,0:T(8,128)(2,1)S(1)} %collective-permute-done.1.refs_2_, bf16[512,512]{1,0:T(8,128)(2,1)S(1)} %collective-permute-done.2.refs_3_, ...), custom_call_target="tpu_custom_call" | custom-call | flops 5368709120 | bytes 17301504 | tf_op jit(solution)/shard_map/pallas_call | solution.py:93
  128.6 7.4 %collective-permute-start.33 = (f32[1280,512]{1,0:T(8,128)S(1)}, f32[1280,512]{1,0:T(8,128)S(1)}, u32[]{:S(2)}, u32[]{:S(2)}) collective-permute-start(f32[1280,512]{1,0:T(8,128)S(1)} %shard_map.29), channel_id=1, source_target_pairs={{0,2},{2,0},{1,3},{3,1},{4,6},{6,4},{5,7},{7,5},{8,10},{10,8},{9,1... | collective-permute-start | bytes 7864328 | tf_op jit(solution)/shard_map/ppermute | solution.py:177
  136.0 2.7 %collective-permute-start.23 = (bf16[512,512]{1,0:T(8,128)(2,1)S(1)}, bf16[512,512]{1,0:T(8,128)(2,1)S(1)}, u32[]{:S(2)}, u32[]{:S(2)}) collective-permute-start(bf16[512,512]{1,0:T(8,128)(2,1)S(1)} %get-tuple-element.6.refs_24_), channel_id=1, source_target_pairs={{0,192},{64,0},{128,64},{192,128},{1,193},{65,1},{129,65},{193,129... | collective-permute-start | bytes 1572872 | tf_op jit(solution)/shard_map/ppermute | solution.py:126
  138.6 11.9 %collective-permute-done.25.refs_30_ = bf16[512,512]{1,0:T(8,128)(2,1)S(1)} collective-permute-done((bf16[512,512]{1,0:T(8,128)(2,1)S(1)}, bf16[512,512]{1,0:T(8,128)(2,1)S(1)}, u32[]{:S(2)}, u32[]{:S(2)}) %collective-permute-start.25) | collective-permute-done | bytes 524320 | tf_op jit(solution)/shard_map/ppermute | solution.py:123
  150.6 13.7 %collective-permute-done.26.refs_28_ = bf16[512,512]{1,0:T(8,128)(2,1)S(1)} collective-permute-done((bf16[512,512]{1,0:T(8,128)(2,1)S(1)}, bf16[512,512]{1,0:T(8,128)(2,1)S(1)}, u32[]{:S(2)}, u32[]{:S(2)}) %collective-permute-start.26) | collective-permute-done | bytes 524320 | tf_op jit(solution)/shard_map/ppermute | solution.py:123
  164.3 16.9 %shard_map.28 = f32[1280,512]{1,0:T(8,128)S(1)} custom-call(bf16[512,512]{1,0:T(8,128)(2,1)S(1)} %slice.3.refs_0_, bf16[512,512]{1,0:T(8,128)(2,1)S(1)} %collective-permute-done.refs_1_, bf16[512,512]{1,0:T(8,128)(2,1)S(1)} %collective-permute-done.1.refs_2_, bf16[512,512]{1,0:T(8,128)(2,1)S(1)} %collective-permute-done.2.refs_3_, ...), custom_call_target="tpu_custom_call" | custom-call | flops 5368709120 | bytes 17301504 | tf_op jit(solution)/shard_map/pallas_call | solution.py:93
  181.2 1.5 add_convert_fusion
  (28 shorter events, 0.1 us)
Async XLA Ops:
  1.2 15.8 %collective-permute-start.11 = (bf16[384,512]{1,0:T(8,128)(2,1)S(1)}, bf16[384,512]{1,0:T(8,128)(2,1)S(1)}, u32[]{:S(2)}, u32[]{:S(2)}) collective-permute-start(bf16[384,512]{1,0:T(8,128)(2,1)S(1)} %get-tuple-element.9.refs_8_), channel_id=1, source_target_pairs={{0,4},{4,8},{8,12},{12,16},{16,20},{20,24},{24,28},{28,0},{1,5},{5... | collective-permute-start | bytes 1179656 | tf_op jit(solution)/shard_map/ppermute | solution.py:123
  3.7 16.0 %collective-permute-start.7 = (bf16[384,512]{1,0:T(8,128)(2,1)S(1)}, bf16[384,512]{1,0:T(8,128)(2,1)S(1)}, u32[]{:S(2)}, u32[]{:S(2)}) collective-permute-start(bf16[384,512]{1,0:T(8,128)(2,1)S(1)} %get-tuple-element.9.refs_8_), channel_id=1, source_target_pairs={{0,28},{4,0},{8,4},{12,8},{16,12},{20,16},{24,20},{28,24},{1,29},{... | collective-permute-start | bytes 1179656 | tf_op jit(solution)/shard_map/ppermute | solution.py:126
  8.8 18.9 %collective-permute-start.3 = (bf16[512,512]{1,0:T(8,128)(2,1)S(1)}, bf16[512,512]{1,0:T(8,128)(2,1)S(1)}, u32[]{:S(2)}, u32[]{:S(2)}) collective-permute-start(bf16[512,512]{1,0:T(8,128)(2,1)S(1)} %slice.3.refs_0_), channel_id=1, source_target_pairs={{0,4},{4,8},{8,12},{12,16},{16,20},{20,24},{24,28},{28,0},{1,5},{5... | collective-permute-start | bytes 1572872 | tf_op jit(solution)/shard_map/ppermute | solution.py:123
  8.9 22.7 %collective-permute-start = (bf16[512,512]{1,0:T(8,128)(2,1)S(1)}, bf16[512,512]{1,0:T(8,128)(2,1)S(1)}, u32[]{:S(2)}, u32[]{:S(2)}) collective-permute-start(bf16[512,512]{1,0:T(8,128)(2,1)S(1)} %slice.3.refs_0_), channel_id=1, source_target_pairs={{0,28},{4,0},{8,4},{12,8},{16,12},{20,16},{24,20},{28,24},{1,29},{... | collective-permute-start | bytes 1572872 | tf_op jit(solution)/shard_map/ppermute | solution.py:126
  13.0 18.5 %collective-permute-start.22 = (bf16[512,512]{1,0:T(8,128)(2,1)S(1)}, bf16[512,512]{1,0:T(8,128)(2,1)S(1)}, u32[]{:S(2)}, u32[]{:S(2)}) collective-permute-start(bf16[512,512]{1,0:T(8,128)(2,1)S(1)} %get-tuple-element.7), channel_id=1, source_target_pairs={{0,35},{1,34},{2,33},{3,32},{32,3},{33,2},{34,1},{35,0},{4,39},{5,... | collective-permute-start | bytes 1572872 | tf_op jit(solution)/shard_map/ppermute | solution.py:159
  17.0 17.4 %collective-permute-start.31 = (bf16[512,512]{1,0:T(8,128)(2,1)S(1)}, bf16[512,512]{1,0:T(8,128)(2,1)S(1)}, u32[]{:S(2)}, u32[]{:S(2)}) collective-permute-start(bf16[512,512]{1,0:T(8,128)(2,1)S(1)} %get-tuple-element.5), channel_id=1, source_target_pairs={{0,66},{2,64},{64,130},{66,128},{128,194},{130,192},{192,2},{194,0... | collective-permute-start | bytes 1572872 | tf_op jit(solution)/shard_map/ppermute | solution.py:132
  19.7 14.7 %collective-permute-start.21 = (bf16[512,512]{1,0:T(8,128)(2,1)S(1)}, bf16[512,512]{1,0:T(8,128)(2,1)S(1)}, u32[]{:S(2)}, u32[]{:S(2)}) collective-permute-start(bf16[512,512]{1,0:T(8,128)(2,1)S(1)} %get-tuple-element.6.refs_24_), channel_id=1, source_target_pairs={{0,32},{32,0},{1,33},{33,1},{2,34},{34,2},{3,35},{35,3},{4,36},{36... | collective-permute-start | bytes 1572872 | tf_op jit(solution)/shard_map/ppermute | solution.py:158
  27.7 15.1 %collective-permute-start.30 = (bf16[512,512]{1,0:T(8,128)(2,1)S(1)}, bf16[512,512]{1,0:T(8,128)(2,1)S(1)}, u32[]{:S(2)}, u32[]{:S(2)}) collective-permute-start(bf16[512,512]{1,0:T(8,128)(2,1)S(1)} %get-tuple-element.5), channel_id=1, source_target_pairs={{0,194},{2,192},{64,2},{66,0},{128,66},{130,64},{192,130},{194,128... | collective-permute-start | bytes 1572872 | tf_op jit(solution)/shard_map/ppermute | solution.py:132
  31.6 14.0 %collective-permute-start.29 = (bf16[512,512]{1,0:T(8,128)(2,1)S(1)}, bf16[512,512]{1,0:T(8,128)(2,1)S(1)}, u32[]{:S(2)}, u32[]{:S(2)}) collective-permute-start(bf16[512,512]{1,0:T(8,128)(2,1)S(1)} %get-tuple-element.5), channel_id=1, source_target_pairs={{0,2},{2,0},{1,3},{3,1},{4,6},{6,4},{5,7},{7,5},{8,10},{10,8},{9,1... | collective-permute-start | bytes 1572872 | tf_op jit(solution)/shard_map/ppermute | solution.py:160
  31.6 14.9 %collective-permute-start.20 = (bf16[384,512]{1,0:T(8,128)(2,1)S(1)}, bf16[384,512]{1,0:T(8,128)(2,1)S(1)}, u32[]{:S(2)}, u32[]{:S(2)}) collective-permute-start(bf16[384,512]{1,0:T(8,128)(2,1)S(1)} %collective-permute-done.11.refs_15_), channel_id=1, source_target_pairs={{0,1},{1,0},{2,3},{3,2},{4,5},{5,4},{6,7},{7,6},{8,9},{9,8},{10,11... | collective-permute-start | bytes 1179656 | tf_op jit(solution)/shard_map/ppermute | solution.py:153
  34.4 12.7 %collective-permute-start.12 = (bf16[384,512]{1,0:T(8,128)(2,1)S(1)}, bf16[384,512]{1,0:T(8,128)(2,1)S(1)}, u32[]{:S(2)}, u32[]{:S(2)}) collective-permute-start(bf16[384,512]{1,0:T(8,128)(2,1)S(1)} %collective-permute-done.11.refs_15_), channel_id=1, source_target_pairs={{0,4},{4,8},{8,12},{12,16},{16,20},{20,24},{24,28},{28,0},{1,5},{5... | collective-permute-start | bytes 1179656 | tf_op jit(solution)/shard_map/ppermute | solution.py:123
  34.4 17.4 %collective-permute-start.14 = (bf16[384,512]{1,0:T(8,128)(2,1)S(1)}, bf16[384,512]{1,0:T(8,128)(2,1)S(1)}, u32[]{:S(2)}, u32[]{:S(2)}) collective-permute-start(bf16[384,512]{1,0:T(8,128)(2,1)S(1)} %collective-permute-done.7.refs_9_), channel_id=1, source_target_pairs={{0,1},{1,0},{2,3},{3,2},{4,5},{5,4},{6,7},{7,6},{8,9},{9,8},{10,11... | collective-permute-start | bytes 1179656 | tf_op jit(solution)/shard_map/ppermute | solution.py:153
  42.8 33.3 %collective-permute-start.24 = (bf16[512,1024]{1,0:T(8,128)(2,1)S(1)}, bf16[512,1024]{1,0:T(8,128)(2,1)S(1)}, u32[]{:S(2)}, u32[]{:S(2)}) collective-permute-start(bf16[512,1024]{1,0:T(8,128)(2,1)S(1)} %constant_dynamic-update-slice_fusion.refs_25_), channel_id=1, source_target_pairs={{0,192},{64,0},{128,64},{192,128},{1,193},{65,1},{129,65},{193,129... | collective-permute-start | bytes 3145736 | tf_op jit(solution)/shard_map/ppermute | solution.py:126
  45.6 9.4 %collective-permute-start.8 = (bf16[384,512]{1,0:T(8,128)(2,1)S(1)}, bf16[384,512]{1,0:T(8,128)(2,1)S(1)}, u32[]{:S(2)}, u32[]{:S(2)}) collective-permute-start(bf16[384,512]{1,0:T(8,128)(2,1)S(1)} %collective-permute-done.7.refs_9_), channel_id=1, source_target_pairs={{0,28},{4,0},{8,4},{12,8},{16,12},{20,16},{24,20},{28,24},{1,29},{... | collective-permute-start | bytes 1179656 | tf_op jit(solution)/shard_map/ppermute | solution.py:126
  46.5 12.9 %collective-permute-start.4 = (bf16[512,512]{1,0:T(8,128)(2,1)S(1)}, bf16[512,512]{1,0:T(8,128)(2,1)S(1)}, u32[]{:S(2)}, u32[]{:S(2)}) collective-permute-start(bf16[512,512]{1,0:T(8,128)(2,1)S(1)} %collective-permute-done.3.refs_7_), channel_id=1, source_target_pairs={{0,4},{4,8},{8,12},{12,16},{16,20},{20,24},{24,28},{28,0},{1,5},{5... | collective-permute-start | bytes 1572872 | tf_op jit(solution)/shard_map/ppermute | solution.py:123
  47.1 19.2 %collective-permute-start.1 = (bf16[512,512]{1,0:T(8,128)(2,1)S(1)}, bf16[512,512]{1,0:T(8,128)(2,1)S(1)}, u32[]{:S(2)}, u32[]{:S(2)}) collective-permute-start(bf16[512,512]{1,0:T(8,128)(2,1)S(1)} %collective-permute-done.refs_1_), channel_id=1, source_target_pairs={{0,28},{4,0},{8,4},{12,8},{16,12},{20,16},{24,20},{28,24},{1,29},{... | collective-permute-start | bytes 1572872 | tf_op jit(solution)/shard_map/ppermute | solution.py:126
  51.8 14.4 %collective-permute-start.32 = (bf16[512,512]{1,0:T(8,128)(2,1)S(1)}, bf16[512,512]{1,0:T(8,128)(2,1)S(1)}, u32[]{:S(2)}, u32[]{:S(2)}) collective-permute-start(bf16[512,512]{1,0:T(8,128)(2,1)S(1)} %collective-permute-done.31.refs_30_), channel_id=1, source_target_pairs={{0,64},{64,128},{128,192},{192,0},{1,65},{65,129},{129,193},{193,1... | collective-permute-start | bytes 1572872 | tf_op jit(solution)/shard_map/ppermute | solution.py:123
  55.0 14.0 %collective-permute-start.19 = (bf16[384,512]{1,0:T(8,128)(2,1)S(1)}, bf16[384,512]{1,0:T(8,128)(2,1)S(1)}, u32[]{:S(2)}, u32[]{:S(2)}) collective-permute-start(bf16[384,512]{1,0:T(8,128)(2,1)S(1)} %collective-permute-done.12.refs_14_), channel_id=1, source_target_pairs={{0,1},{1,0},{2,3},{3,2},{4,5},{5,4},{6,7},{7,6},{8,9},{9,8},{10,11... | collective-permute-start | bytes 1179656 | tf_op jit(solution)/shard_map/ppermute | solution.py:153
  59.4 31.2 %collective-permute-start.28 = (bf16[512,1024]{1,0:T(8,128)(2,1)S(1)}, bf16[512,1024]{1,0:T(8,128)(2,1)S(1)}, u32[]{:S(2)}, u32[]{:S(2)}) collective-permute-start(bf16[512,1024]{1,0:T(8,128)(2,1)S(1)} %constant_dynamic-update-slice_fusion.refs_25_), channel_id=1, source_target_pairs={{0,64},{64,128},{128,192},{192,0},{1,65},{65,129},{129,193},{193,1... | collective-permute-start | bytes 3145736 | tf_op jit(solution)/shard_map/ppermute | solution.py:123
  66.3 9.8 %collective-permute-start.13 = (bf16[384,512]{1,0:T(8,128)(2,1)S(1)}, bf16[384,512]{1,0:T(8,128)(2,1)S(1)}, u32[]{:S(2)}, u32[]{:S(2)}) collective-permute-start(bf16[384,512]{1,0:T(8,128)(2,1)S(1)} %collective-permute-done.12.refs_14_), channel_id=1, source_target_pairs={{0,4},{4,8},{8,12},{12,16},{16,20},{20,24},{24,28},{28,0},{1,5},{5... | collective-permute-start | bytes 1179656 | tf_op jit(solution)/shard_map/ppermute | solution.py:123
  66.3 10.6 %collective-permute-start.15 = (bf16[384,512]{1,0:T(8,128)(2,1)S(1)}, bf16[384,512]{1,0:T(8,128)(2,1)S(1)}, u32[]{:S(2)}, u32[]{:S(2)}) collective-permute-start(bf16[384,512]{1,0:T(8,128)(2,1)S(1)} %collective-permute-done.8.refs_10_), channel_id=1, source_target_pairs={{0,1},{1,0},{2,3},{3,2},{4,5},{5,4},{6,7},{7,6},{8,9},{9,8},{10,11... | collective-permute-start | bytes 1179656 | tf_op jit(solution)/shard_map/ppermute | solution.py:153
  69.0 10.5 %collective-permute-start.9 = (bf16[384,512]{1,0:T(8,128)(2,1)S(1)}, bf16[384,512]{1,0:T(8,128)(2,1)S(1)}, u32[]{:S(2)}, u32[]{:S(2)}) collective-permute-start(bf16[384,512]{1,0:T(8,128)(2,1)S(1)} %collective-permute-done.8.refs_10_), channel_id=1, source_target_pairs={{0,28},{4,0},{8,4},{12,8},{16,12},{20,16},{24,20},{28,24},{1,29},{... | collective-permute-start | bytes 1179656 | tf_op jit(solution)/shard_map/ppermute | solution.py:126
  76.1 11.7 %collective-permute-start.5 = (bf16[512,512]{1,0:T(8,128)(2,1)S(1)}, bf16[512,512]{1,0:T(8,128)(2,1)S(1)}, u32[]{:S(2)}, u32[]{:S(2)}) collective-permute-start(bf16[512,512]{1,0:T(8,128)(2,1)S(1)} %collective-permute-done.4.refs_6_), channel_id=1, source_target_pairs={{0,4},{4,8},{8,12},{12,16},{16,20},{20,24},{24,28},{28,0},{1,5},{5... | collective-permute-start | bytes 1572872 | tf_op jit(solution)/shard_map/ppermute | solution.py:123
  76.1 35.4 %collective-permute-start.27 = (bf16[512,1024]{1,0:T(8,128)(2,1)S(1)}, bf16[512,1024]{1,0:T(8,128)(2,1)S(1)}, u32[]{:S(2)}, u32[]{:S(2)}) collective-permute-start(bf16[512,1024]{1,0:T(8,128)(2,1)S(1)} %collective-permute-done.24.refs_27_), channel_id=1, source_target_pairs={{0,192},{64,0},{128,64},{192,128},{1,193},{65,1},{129,65},{193,129... | collective-permute-start | bytes 3145736 | tf_op jit(solution)/shard_map/ppermute | solution.py:126
  76.9 11.9 %collective-permute-start.2 = (bf16[512,512]{1,0:T(8,128)(2,1)S(1)}, bf16[512,512]{1,0:T(8,128)(2,1)S(1)}, u32[]{:S(2)}, u32[]{:S(2)}) collective-permute-start(bf16[512,512]{1,0:T(8,128)(2,1)S(1)} %collective-permute-done.1.refs_2_), channel_id=1, source_target_pairs={{0,28},{4,0},{8,4},{12,8},{16,12},{20,16},{24,20},{28,24},{1,29},{... | collective-permute-start | bytes 1572872 | tf_op jit(solution)/shard_map/ppermute | solution.py:126
  79.6 17.7 %collective-permute-start.10 = (bf16[384,512]{1,0:T(8,128)(2,1)S(1)}, bf16[384,512]{1,0:T(8,128)(2,1)S(1)}, u32[]{:S(2)}, u32[]{:S(2)}) collective-permute-start(bf16[384,512]{1,0:T(8,128)(2,1)S(1)} %collective-permute-done.9.refs_11_), channel_id=1, source_target_pairs={{0,28},{4,0},{8,4},{12,8},{16,12},{20,16},{24,20},{28,24},{1,29},{... | collective-permute-start | bytes 1179656 | tf_op jit(solution)/shard_map/ppermute | solution.py:126
  87.8 23.6 %collective-permute-start.6 = (bf16[512,512]{1,0:T(8,128)(2,1)S(1)}, bf16[512,512]{1,0:T(8,128)(2,1)S(1)}, u32[]{:S(2)}, u32[]{:S(2)}) collective-permute-start(bf16[512,512]{1,0:T(8,128)(2,1)S(1)} %collective-permute-done.5.refs_5_), channel_id=1, source_target_pairs={{0,4},{4,8},{8,12},{12,16},{16,20},{20,24},{24,28},{28,0},{1,5},{5... | collective-permute-start | bytes 1572872 | tf_op jit(solution)/shard_map/ppermute | solution.py:123
  88.8 14.2 %collective-permute-start.16 = (bf16[384,512]{1,0:T(8,128)(2,1)S(1)}, bf16[384,512]{1,0:T(8,128)(2,1)S(1)}, u32[]{:S(2)}, u32[]{:S(2)}) collective-permute-start(bf16[384,512]{1,0:T(8,128)(2,1)S(1)} %collective-permute-done.9.refs_11_), channel_id=1, source_target_pairs={{0,1},{1,0},{2,3},{3,2},{4,5},{5,4},{6,7},{7,6},{8,9},{9,8},{10,11... | collective-permute-start | bytes 1179656 | tf_op jit(solution)/shard_map/ppermute | solution.py:153
  90.6 12.4 %collective-permute-start.18 = (bf16[384,512]{1,0:T(8,128)(2,1)S(1)}, bf16[384,512]{1,0:T(8,128)(2,1)S(1)}, u32[]{:S(2)}, u32[]{:S(2)}) collective-permute-start(bf16[384,512]{1,0:T(8,128)(2,1)S(1)} %collective-permute-done.13.refs_13_), channel_id=1, source_target_pairs={{0,1},{1,0},{2,3},{3,2},{4,5},{5,4},{6,7},{7,6},{8,9},{9,8},{10,11... | collective-permute-start | bytes 1179656 | tf_op jit(solution)/shard_map/ppermute | solution.py:153
  97.3 14.2 %collective-permute-start.17 = (bf16[384,512]{1,0:T(8,128)(2,1)S(1)}, bf16[384,512]{1,0:T(8,128)(2,1)S(1)}, u32[]{:S(2)}, u32[]{:S(2)}) collective-permute-start(bf16[384,512]{1,0:T(8,128)(2,1)S(1)} %collective-permute-done.10.refs_12_), channel_id=1, source_target_pairs={{0,1},{1,0},{2,3},{3,2},{4,5},{5,4},{6,7},{7,6},{8,9},{9,8},{10,11... | collective-permute-start | bytes 1179656 | tf_op jit(solution)/shard_map/ppermute | solution.py:153
  128.6 52.7 %collective-permute-start.33 = (f32[1280,512]{1,0:T(8,128)S(1)}, f32[1280,512]{1,0:T(8,128)S(1)}, u32[]{:S(2)}, u32[]{:S(2)}) collective-permute-start(f32[1280,512]{1,0:T(8,128)S(1)} %shard_map.29), channel_id=1, source_target_pairs={{0,2},{2,0},{1,3},{3,1},{4,6},{6,4},{5,7},{7,5},{8,10},{10,8},{9,1... | collective-permute-start | bytes 7864328 | tf_op jit(solution)/shard_map/ppermute | solution.py:177
  136.0 14.6 %collective-permute-start.25 = (bf16[512,512]{1,0:T(8,128)(2,1)S(1)}, bf16[512,512]{1,0:T(8,128)(2,1)S(1)}, u32[]{:S(2)}, u32[]{:S(2)}) collective-permute-start(bf16[512,512]{1,0:T(8,128)(2,1)S(1)} %get-tuple-element.6.refs_24_), channel_id=1, source_target_pairs={{0,64},{64,128},{128,192},{192,0},{1,65},{65,129},{129,193},{193,1... | collective-permute-start | bytes 1572872 | tf_op jit(solution)/shard_map/ppermute | solution.py:123
  136.0 14.6 %collective-permute-start.23 = (bf16[512,512]{1,0:T(8,128)(2,1)S(1)}, bf16[512,512]{1,0:T(8,128)(2,1)S(1)}, u32[]{:S(2)}, u32[]{:S(2)}) collective-permute-start(bf16[512,512]{1,0:T(8,128)(2,1)S(1)} %get-tuple-element.6.refs_24_), channel_id=1, source_target_pairs={{0,192},{64,0},{128,64},{192,128},{1,193},{65,1},{129,65},{193,129... | collective-permute-start | bytes 1572872 | tf_op jit(solution)/shard_map/ppermute | solution.py:126
  150.6 13.7 %collective-permute-start.26 = (bf16[512,512]{1,0:T(8,128)(2,1)S(1)}, bf16[512,512]{1,0:T(8,128)(2,1)S(1)}, u32[]{:S(2)}, u32[]{:S(2)}) collective-permute-start(bf16[512,512]{1,0:T(8,128)(2,1)S(1)} %collective-permute-done.25.refs_30_), channel_id=1, source_target_pairs={{0,64},{64,128},{128,192},{192,0},{1,65},{65,129},{129,193},{193,1... | collective-permute-start | bytes 1572872 | tf_op jit(solution)/shard_map/ppermute | solution.py:123
